TPU v7x, 32 devices: a whole 2x2x4 slice. The times are simulated.
32 devices in a mesh: dp: 4 (over z), expert: 8 (over y, x, core).
Axes of the slice: x: 2, y: 2, z: 4, core: 2. Of those that a mesh axis runs over, the one named last changes fastest.
Arguments:
- hidden: bfloat16 [4, 1024, 2048], P('dp', 'expert'), may hold values from -6 to 6
- output_cotangent: bfloat16 [4, 1024, 2048], P('dp', 'expert'), may hold values from -6 to 6
- attention_gain: float32 [2048], replicated, may hold values from 0.5 to 1.5
- expert_norm_gain: float32 [2048], replicated, may hold values from 0.5 to 1.5
- query_key_value_weight: bfloat16 [3, 2048, 2048], P(None, None, 'expert'), may hold values from -0.125 to 0.125
- output_weight: bfloat16 [2048, 2048], P('expert'), may hold values from -0.5 to 0.5
- gate_up_weight: bfloat16 [16, 2, 2048, 1024], P('expert'), may hold values from -0.125 to 0.125
- down_weight: bfloat16 [16, 1024, 2048], P('expert'), may hold values from -0.1875 to 0.1875
- token_experts: int32 [4, 1024, 8], P('dp', 'expert'), may hold values from 0 to 15, all different within a row; in each aligned block of 128 rows (0 to 127, 128 to 255, ..., all dimensions but the last counted through in order) at most 80 rows name the same one
- expert_gate_weight: float32 [4, 1024, 8], P('dp', 'expert'), may hold values from 0.05 to 0.25
- sequence_adapter: int32 [4], replicated, may hold values from 0 to 7
- optimizer_steps: int32 [1], replicated, may hold values from 1 to 20
- adapter_attention_input: bfloat16 [3, 8, 16, 2048], replicated, may hold values from -0.125 to 0.125
- adapter_attention_output: bfloat16 [3, 8, 16, 2048], P(None, None, None, 'expert'), may hold values from -0.375 to 0.375
- adapter_projection_input: bfloat16 [8, 16, 2048], P(None, None, 'expert'), may hold values from -0.5 to 0.5
- adapter_projection_output: bfloat16 [8, 16, 2048], replicated, may hold values from -0.375 to 0.375
- adapter_hidden_input: bfloat16 [16, 2, 8, 16, 2048], P('expert'), may hold values from -0.125 to 0.125
- adapter_hidden_output: bfloat16 [16, 2, 8, 16, 1024], P('expert'), may hold values from -0.375 to 0.375
- adapter_down_input: bfloat16 [16, 8, 16, 1024], P('expert'), may hold values from -0.1875 to 0.1875
- adapter_down_output: bfloat16 [16, 8, 16, 2048], P('expert'), may hold values from -0.375 to 0.375
- moment_attention_input: float32 [3, 8, 16, 2048], P(None, None, None, ('dp', 'expert')), may hold values from -0.036 to 0.036
- moment_attention_output: float32 [3, 8, 16, 2048], P(None, None, None, ('expert', 'dp')), may hold values from -0.036 to 0.036
- moment_projection_input: float32 [8, 16, 2048], P(None, None, ('expert', 'dp')), may hold values from -0.036 to 0.036
- moment_projection_output: float32 [8, 16, 2048], P(None, None, ('dp', 'expert')), may hold values from -0.036 to 0.036
- moment_hidden_input: float32 [16, 2, 8, 16, 2048], P('expert', None, None, None, 'dp'), may hold values from -0.036 to 0.036
- moment_hidden_output: float32 [16, 2, 8, 16, 1024], P('expert', None, None, None, 'dp'), may hold values from -0.036 to 0.036
- moment_down_input: float32 [16, 8, 16, 1024], P('expert', None, None, 'dp'), may hold values from -0.036 to 0.036
- moment_down_output: float32 [16, 8, 16, 2048], P('expert', None, None, 'dp'), may hold values from -0.036 to 0.036
- squared_attention_input: float32 [3, 8, 16, 2048], P(None, None, None, ('dp', 'expert')), may hold values from 2e-05 to 0.001
- squared_attention_output: float32 [3, 8, 16, 2048], P(None, None, None, ('expert', 'dp')), may hold values from 2e-05 to 0.001
- squared_projection_input: float32 [8, 16, 2048], P(None, None, ('expert', 'dp')), may hold values from 2e-05 to 0.001
- squared_projection_output: float32 [8, 16, 2048], P(None, None, ('dp', 'expert')), may hold values from 2e-05 to 0.001
- squared_hidden_input: float32 [16, 2, 8, 16, 2048], P('expert', None, None, None, 'dp'), may hold values from 2e-05 to 0.001
- squared_hidden_output: float32 [16, 2, 8, 16, 1024], P('expert', None, None, None, 'dp'), may hold values from 2e-05 to 0.001
- squared_down_input: float32 [16, 8, 16, 1024], P('expert', None, None, 'dp'), may hold values from 2e-05 to 0.001
- squared_down_output: float32 [16, 8, 16, 2048], P('expert', None, None, 'dp'), may hold values from 2e-05 to 0.001
Outputs:
- block_out: bfloat16 [4, 1024, 2048], P('dp', 'expert')
- grad_hidden: float32 [4, 1024, 2048], P('dp', 'expert')
- global_norm: float32 [1], replicated
- grad_qkv_a: float32 [3, 8, 16, 2048], P(None, None, None, ('dp', 'expert'))
- new_first_qkv_a: float32 [3, 8, 16, 2048], P(None, None, None, ('dp', 'expert'))
- new_second_qkv_a: float32 [3, 8, 16, 2048], P(None, None, None, ('dp', 'expert'))
- update_qkv_a: float32 [3, 8, 16, 2048], P(None, None, None, ('dp', 'expert'))
- grad_qkv_b: float32 [3, 8, 16, 2048], P(None, None, None, ('expert', 'dp'))
- new_first_qkv_b: float32 [3, 8, 16, 2048], P(None, None, None, ('expert', 'dp'))
- new_second_qkv_b: float32 [3, 8, 16, 2048], P(None, None, None, ('expert', 'dp'))
- update_qkv_b: float32 [3, 8, 16, 2048], P(None, None, None, ('expert', 'dp'))
- grad_out_a: float32 [8, 16, 2048], P(None, None, ('expert', 'dp'))
- new_first_out_a: float32 [8, 16, 2048], P(None, None, ('expert', 'dp'))
- new_second_out_a: float32 [8, 16, 2048], P(None, None, ('expert', 'dp'))
- update_out_a: float32 [8, 16, 2048], P(None, None, ('expert', 'dp'))
- grad_out_b: float32 [8, 16, 2048], P(None, None, ('dp', 'expert'))
- new_first_out_b: float32 [8, 16, 2048], P(None, None, ('dp', 'expert'))
- new_second_out_b: float32 [8, 16, 2048], P(None, None, ('dp', 'expert'))
- update_out_b: float32 [8, 16, 2048], P(None, None, ('dp', 'expert'))
- grad_in_a: float32 [16, 2, 8, 16, 2048], P('expert', None, None, None, 'dp')
- new_first_in_a: float32 [16, 2, 8, 16, 2048], P('expert', None, None, None, 'dp')
- new_second_in_a: float32 [16, 2, 8, 16, 2048], P('expert', None, None, None, 'dp')
- update_in_a: float32 [16, 2, 8, 16, 2048], P('expert', None, None, None, 'dp')
- grad_mid_b: float32 [16, 2, 8, 16, 1024], P('expert', None, None, None, 'dp')
- new_first_mid_b: float32 [16, 2, 8, 16, 1024], P('expert', None, None, None, 'dp')
- new_second_mid_b: float32 [16, 2, 8, 16, 1024], P('expert', None, None, None, 'dp')
- update_mid_b: float32 [16, 2, 8, 16, 1024], P('expert', None, None, None, 'dp')
- grad_down_a: float32 [16, 8, 16, 1024], P('expert', None, None, 'dp')
- new_first_down_a: float32 [16, 8, 16, 1024], P('expert', None, None, 'dp')
- new_second_down_a: float32 [16, 8, 16, 1024], P('expert', None, None, 'dp')
- update_down_a: float32 [16, 8, 16, 1024], P('expert', None, None, 'dp')
- grad_down_b: float32 [16, 8, 16, 2048], P('expert', None, None, 'dp')
- new_first_down_b: float32 [16, 8, 16, 2048], P('expert', None, None, 'dp')
- new_second_down_b: float32 [16, 8, 16, 2048], P('expert', None, None, 'dp')
- update_down_b: float32 [16, 8, 16, 2048], P('expert', None, None, 'dp')
Inputs may be any that keep to these rules, and one draw needn't show every extreme that they name: `token_experts`: in each aligned block of 128 positions (the rows of one device) no expert is named by more than 80 assignments; this bound is reached in some block.
All inputs are finite; a program needn't handle non-finite values.
Results may differ from a plain program's by a relative error of at most 0.02.
Values may be sent and summed in bfloat16 or wider, within the bound.
A program may use at most 256 MiB of HBM per device.

v0:
```python
import jax
import jax.numpy as jnp
from jax import lax
from jax.sharding import PartitionSpec as P

MODEL_WIDTH = 2048
HEAD = 128
TOP = 8
ADAPTER_COUNT = 8
EXP_DEV = 2
CLIP = 256


norm_eps = 1e-05
beta_one = 0.9
beta_two = 0.95
learn_rate = 0.02
weight_decay = 0.1
adam_eps = 1e-08
highest = lax.Precision.HIGHEST
single = jnp.float32
brain = jnp.bfloat16


def rms_scale(values, gain):
    return values * lax.rsqrt(jnp.mean(values * values, axis=-1, keepdims=True) + norm_eps) * gain


def norm_back(values, gain, grad):
    inverse = lax.rsqrt(jnp.mean(values * values, axis=-1, keepdims=True) + norm_eps)
    scaled = grad * gain
    return inverse * scaled - values * inverse * inverse * inverse * jnp.mean(
        scaled * values, axis=-1, keepdims=True
    )


def select_adapter(array, adapter_slot, axis):
    return lax.dynamic_index_in_dim(array, adapter_slot, axis, keepdims=False)


def spread_out(compact, marker, axis):
    shape = [1] * (compact.ndim + 1)
    shape[axis] = marker.shape[0]
    return jnp.expand_dims(compact, axis) * marker.reshape(shape)


def local_portion(weight, piece_index, pieces):
    width = weight.shape[-1] // pieces
    return lax.dynamic_slice_in_dim(weight, piece_index * width, width, weight.ndim - 1).astype(
        single
    )


def adam_step(grad, weight, first, second, factor_array, step_number):
    clipped = grad * factor_array
    first_new = beta_one * first + (1.0 - beta_one) * clipped
    second_new = beta_two * second + (1.0 - beta_two) * clipped * clipped
    fix_first = 1.0 - jnp.power(beta_one, step_number)
    fix_second = 1.0 - jnp.power(beta_two, step_number)
    update = -learn_rate * (
        first_new / fix_first / (jnp.sqrt(second_new / fix_second) + adam_eps)
        + weight_decay * weight
    )
    return (first_new, second_new, update)


def per_device(
    hidden,
    output_cotangent,
    attention_gain,
    expert_norm_gain,
    query_key_value_weight,
    output_weight,
    gate_up_weight,
    down_weight,
    token_experts,
    expert_gate_weight,
    sequence_adapter,
    optimizer_steps,
    adapter_attention_input,
    adapter_attention_output,
    adapter_projection_input,
    adapter_projection_output,
    adapter_hidden_input,
    adapter_hidden_output,
    adapter_down_input,
    adapter_down_output,
    moment_attention_input,
    moment_attention_output,
    moment_projection_input,
    moment_projection_output,
    moment_hidden_input,
    moment_hidden_output,
    moment_down_input,
    moment_down_output,
    squared_attention_input,
    squared_attention_output,
    squared_projection_input,
    squared_projection_output,
    squared_hidden_input,
    squared_hidden_output,
    squared_down_input,
    squared_down_output,
):
    group_list = lax.axis_size("expert")
    replica_total = lax.axis_size("dp")
    replica_index = lax.axis_index("dp")
    group_index = lax.axis_index("expert")
    adapter_slot = lax.dynamic_index_in_dim(sequence_adapter, replica_index, 0, keepdims=False)
    tok_dev = hidden.shape[1]
    length = tok_dev * group_list
    width_here = query_key_value_weight.shape[2]
    heads_here = width_here // HEAD
    block = min(512, length)
    nblocks = length // block
    scale = HEAD ** (-0.5)
    experts_all = EXP_DEV * group_list
    cap = min(tok_dev, tok_dev * TOP * 5 // (4 * experts_all))
    picked_projection_input = select_adapter(adapter_projection_input, adapter_slot, 0)
    picked_projection_output = select_adapter(adapter_projection_output, adapter_slot, 0)
    tokens = hidden[0].astype(single)
    normed = rms_scale(tokens, attention_gain).astype(brain)
    sequence = lax.all_gather(normed, "expert", axis=0, tiled=True)
    picked_attention_input = select_adapter(adapter_attention_input, adapter_slot, 1)
    picked_attention_output = select_adapter(adapter_attention_output, adapter_slot, 1)
    low_qkv = jnp.einsum(
        "ld,jrd->jlr", sequence, picked_attention_input, preferred_element_type=single
    ).astype(brain)
    project = jnp.einsum(
        "ld,jde->jle", sequence, query_key_value_weight, preferred_element_type=single
    )
    project = (
        project
        + jnp.einsum(
            "jlr,jre->jle", low_qkv, picked_attention_output, preferred_element_type=single
        )
    ).astype(brain)
    queries = project[0].reshape(length, heads_here, HEAD)
    keys = project[1].reshape(length, heads_here, HEAD)
    values = project[2].reshape(length, heads_here, HEAD)

    def attend(query_block):
        scores = (
            jnp.einsum("bhd,khd->hbk", query_block, keys, preferred_element_type=single) * scale
        )
        peak = jnp.max(scores, axis=-1, keepdims=True)
        expo = jnp.exp(scores - peak)
        totals = jnp.sum(expo, axis=-1, keepdims=True)
        probs = (expo / totals).astype(brain)
        mixed_block = jnp.einsum(
            "hbk,khd->bhd", probs, values, preferred_element_type=single
        ).astype(brain)
        return (mixed_block, (peak + jnp.log(totals))[..., 0])

    query_blocks = queries.reshape(nblocks, block, heads_here, HEAD)
    mixed, log_sums = lax.map(attend, query_blocks)
    mixed = mixed.reshape(length, width_here)
    out_rank = jnp.einsum(
        "le,re->lr", mixed, picked_projection_input, preferred_element_type=single
    )
    ranks = out_rank
    branch = lax.psum_scatter(
        jnp.dot(mixed, output_weight, preferred_element_type=single)
        + jnp.dot(ranks, picked_projection_output.astype(single), precision=highest),
        "expert",
        scatter_dimension=0,
        tiled=True,
    )
    resid = tokens + branch
    moe_in = rms_scale(resid, expert_norm_gain).astype(brain)
    routes = token_experts[0].reshape(-1)
    onehot = (routes[:, None] == jnp.arange(experts_all, dtype=jnp.int32)[None, :]).astype(
        jnp.int32
    )
    within = jnp.sum((jnp.cumsum(onehot, axis=0) - 1) * onehot, axis=1)
    slots = routes % EXP_DEV * (group_list * cap) + routes // EXP_DEV * cap + within
    token_rows = jnp.repeat(jnp.arange(tok_dev, dtype=jnp.int32), TOP)
    outgoing = (
        jnp.zeros((EXP_DEV * group_list * cap, MODEL_WIDTH), brain)
        .at[slots]
        .set(moe_in[token_rows])
    )
    arrived = lax.all_to_all(
        outgoing.reshape(EXP_DEV, group_list * cap, MODEL_WIDTH),
        "expert",
        split_axis=1,
        concat_axis=1,
        tiled=True,
    )
    picked_hidden_input = select_adapter(adapter_hidden_input, adapter_slot, 2)
    picked_hidden_output = select_adapter(adapter_hidden_output, adapter_slot, 2)
    picked_down_input = select_adapter(adapter_down_input, adapter_slot, 1)
    picked_down_output = select_adapter(adapter_down_output, adapter_slot, 1)
    in_rank = jnp.einsum(
        "ecd,ejrd->ejcr", arrived, picked_hidden_input, preferred_element_type=single
    ).astype(brain)
    gate_up = jnp.einsum("ecd,ejdf->ejcf", arrived, gate_up_weight, preferred_element_type=single)
    gate_up = gate_up + jnp.einsum(
        "ejcr,ejrf->ejcf", in_rank, picked_hidden_output, preferred_element_type=single
    )
    sigmoid_gate = jax.nn.sigmoid(gate_up[:, 0])
    swish_gate = gate_up[:, 0] * sigmoid_gate
    active = (swish_gate * gate_up[:, 1]).astype(brain)
    down_rank = jnp.einsum(
        "ecf,erf->ecr", active, picked_down_input, preferred_element_type=single
    ).astype(brain)
    expert_out = jnp.einsum("ecf,efd->ecd", active, down_weight, preferred_element_type=single)
    expert_out = (
        expert_out
        + jnp.einsum("ecr,erd->ecd", down_rank, picked_down_output, preferred_element_type=single)
    ).astype(brain)
    returned = lax.all_to_all(
        expert_out, "expert", split_axis=1, concat_axis=1, tiled=True
    ).reshape(-1, MODEL_WIDTH)
    route_weight = expert_gate_weight[0]
    picked = returned[slots].reshape(tok_dev, TOP, MODEL_WIDTH).astype(single)
    block_out = (resid + jnp.sum(route_weight[:, :, None] * picked, axis=1)).astype(brain)
    grad_top = output_cotangent[0].astype(single)
    grad_copies = (
        (route_weight[:, :, None] * grad_top[:, None, :]).astype(brain).reshape(-1, MODEL_WIDTH)
    )
    outgoing_grad = (
        jnp.zeros((EXP_DEV * group_list * cap, MODEL_WIDTH), brain).at[slots].set(grad_copies)
    )
    grad_expert = lax.all_to_all(
        outgoing_grad.reshape(EXP_DEV, group_list * cap, MODEL_WIDTH),
        "expert",
        split_axis=1,
        concat_axis=1,
        tiled=True,
    )
    grad_down_rank = jnp.einsum(
        "ecd,erd->ecr", grad_expert, picked_down_output, preferred_element_type=single
    ).astype(brain)
    grad_active = jnp.einsum(
        "ecd,efd->ecf", grad_expert, down_weight, preferred_element_type=single
    )
    grad_active = grad_active + jnp.einsum(
        "ecr,erf->ecf", grad_down_rank, picked_down_input, preferred_element_type=single
    )
    grad_active = grad_active.astype(brain).astype(single)
    g_down_b = jnp.einsum("ecr,ecd->erd", down_rank, grad_expert, preferred_element_type=single)
    g_down_a = jnp.einsum("ecr,ecf->erf", grad_down_rank, active, preferred_element_type=single)
    grad_gate = (
        grad_active * gate_up[:, 1] * sigmoid_gate * (1.0 + gate_up[:, 0] * (1.0 - sigmoid_gate))
    )
    grad_up = grad_active * swish_gate
    grad_gate_up = jnp.stack([grad_gate, grad_up], axis=1).astype(brain)
    grad_in_rank = jnp.einsum(
        "ejcf,ejrf->ejcr", grad_gate_up, picked_hidden_output, preferred_element_type=single
    ).astype(brain)
    g_mid_b = jnp.einsum("ejcr,ejcf->ejrf", in_rank, grad_gate_up, preferred_element_type=single)
    g_in_a = jnp.einsum("ejcr,ecd->ejrd", grad_in_rank, arrived, preferred_element_type=single)
    grad_slots = jnp.einsum(
        "ejcf,ejdf->ecd", grad_gate_up, gate_up_weight, preferred_element_type=single
    )
    grad_slots = (
        grad_slots
        + jnp.einsum(
            "ejcr,ejrd->ecd", grad_in_rank, picked_hidden_input, preferred_element_type=single
        )
    ).astype(brain)
    came_back = lax.all_to_all(
        grad_slots, "expert", split_axis=1, concat_axis=1, tiled=True
    ).reshape(-1, MODEL_WIDTH)
    grad_moe_in = jnp.sum(
        came_back[slots].reshape(tok_dev, TOP, MODEL_WIDTH).astype(single), axis=1
    )
    grad_resid = grad_top + norm_back(resid, expert_norm_gain, grad_moe_in)
    grad_branch = grad_resid.astype(brain)
    branch_full = lax.all_gather(grad_branch, "expert", axis=0, tiled=True)
    grad_out_rank = jnp.einsum(
        "ld,rd->lr", branch_full, picked_projection_output, preferred_element_type=single
    )
    grad_mixed = jnp.einsum("ld,ed->le", branch_full, output_weight, preferred_element_type=single)
    grad_mixed = (
        grad_mixed
        + jnp.dot(grad_out_rank, picked_projection_input.astype(single), precision=highest)
    ).astype(brain)
    g_out_b = jnp.einsum("lr,ld->rd", out_rank, branch_full.astype(single), precision=highest)
    g_out_a = jnp.einsum("lr,le->re", grad_out_rank, mixed.astype(single), precision=highest)

    def back_block(carry, items):
        grad_keys, grad_values = carry
        query_block, grad_block, log_block = items
        scores = (
            jnp.einsum("bhd,khd->hbk", query_block, keys, preferred_element_type=single) * scale
        )
        probs = jnp.exp(scores - log_block[..., None])
        grad_probs = jnp.einsum("bhd,khd->hbk", grad_block, values, preferred_element_type=single)
        grad_scores = (
            probs * (grad_probs - jnp.sum(grad_probs * probs, axis=-1, keepdims=True))
        ).astype(brain)
        grad_query = (
            jnp.einsum("hbk,khd->bhd", grad_scores, keys, preferred_element_type=single) * scale
        )
        grad_keys = (
            grad_keys
            + jnp.einsum("hbk,bhd->khd", grad_scores, query_block, preferred_element_type=single)
            * scale
        )
        grad_values = grad_values + jnp.einsum(
            "hbk,bhd->khd", probs.astype(brain), grad_block, preferred_element_type=single
        )
        return ((grad_keys, grad_values), grad_query.astype(brain))

    zeros_heads = jnp.zeros((length, heads_here, HEAD), single)
    grad_blocks = grad_mixed.reshape(nblocks, block, heads_here, HEAD)
    (grad_keys, grad_values), grad_queries = lax.scan(
        back_block, (zeros_heads, zeros_heads), (query_blocks, grad_blocks, log_sums)
    )
    grad_project = jnp.stack(
        [
            grad_queries.reshape(length, width_here),
            grad_keys.reshape(length, width_here).astype(brain),
            grad_values.reshape(length, width_here).astype(brain),
        ],
        axis=0,
    )
    g_qkv_b = jnp.einsum("jlr,jle->jre", low_qkv, grad_project, preferred_element_type=single)
    grad_low = jnp.einsum(
        "jle,jre->jlr", grad_project, picked_attention_output, preferred_element_type=single
    )
    g_qkv_a = jnp.einsum("jlr,ld->jrd", grad_low, sequence.astype(single), precision=highest)
    ranks = grad_low
    grad_normed = lax.psum_scatter(
        (
            jnp.einsum(
                "jle,jde->ld", grad_project, query_key_value_weight, preferred_element_type=single
            )
            + jnp.einsum(
                "jlr,jrd->ld", ranks, picked_attention_input.astype(single), precision=highest
            )
        ).astype(jnp.bfloat16),
        "expert",
        scatter_dimension=0,
        tiled=True,
    ).astype(jnp.float32)
    grad_tokens = grad_resid + norm_back(tokens, attention_gain, grad_normed)
    marker = (jnp.arange(ADAPTER_COUNT, dtype=jnp.int32) == adapter_slot).astype(single)
    sum_qkv_a, sum_out_b = (
        lax.psum_scatter(
            spread_out(g_qkv_a, marker, 1), ("dp", "expert"), scatter_dimension=3, tiled=True
        ),
        lax.psum_scatter(
            spread_out(g_out_b, marker, 0), ("dp", "expert"), scatter_dimension=2, tiled=True
        ),
    )
    sum_qkv_b, sum_out_a, summed_hidden_input, sum_mid_b, sum_down_a, sum_down_b = (
        lax.psum_scatter(
            spread_out(g_qkv_b, marker, 1).astype(jnp.bfloat16),
            "dp",
            scatter_dimension=3,
            tiled=True,
        ).astype(jnp.float32),
        lax.psum_scatter(
            spread_out(g_out_a, marker, 0).astype(jnp.bfloat16),
            "dp",
            scatter_dimension=2,
            tiled=True,
        ).astype(jnp.float32),
        lax.psum_scatter(
            spread_out(g_in_a, marker, 2).astype(jnp.bfloat16),
            "dp",
            scatter_dimension=4,
            tiled=True,
        ).astype(jnp.float32),
        lax.psum_scatter(
            spread_out(g_mid_b, marker, 2).astype(jnp.bfloat16),
            "dp",
            scatter_dimension=4,
            tiled=True,
        ).astype(jnp.float32),
        lax.psum_scatter(
            spread_out(g_down_a, marker, 1).astype(jnp.bfloat16),
            "dp",
            scatter_dimension=3,
            tiled=True,
        ).astype(jnp.float32),
        lax.psum_scatter(
            spread_out(g_down_b, marker, 1).astype(jnp.bfloat16),
            "dp",
            scatter_dimension=3,
            tiled=True,
        ).astype(jnp.float32),
    )
    squares = jnp.zeros((), single)
    for grad in (
        sum_qkv_a,
        sum_qkv_b,
        sum_out_a,
        sum_out_b,
        summed_hidden_input,
        sum_mid_b,
        sum_down_a,
        sum_down_b,
    ):
        squares = squares + jnp.sum(grad * grad)
    norm_value = jnp.sqrt(lax.psum(squares, ("dp", "expert")))
    factor_array = jnp.minimum(1.0, CLIP / norm_value)
    step_number = optimizer_steps[0].astype(single)
    common_index = replica_index * group_list + group_index
    state_qkv_a = adam_step(
        sum_qkv_a,
        local_portion(adapter_attention_input, common_index, replica_total * group_list),
        moment_attention_input,
        squared_attention_input,
        factor_array,
        step_number,
    )
    state_qkv_b = adam_step(
        sum_qkv_b,
        local_portion(adapter_attention_output, replica_index, replica_total),
        moment_attention_output,
        squared_attention_output,
        factor_array,
        step_number,
    )
    state_out_a = adam_step(
        sum_out_a,
        local_portion(adapter_projection_input, replica_index, replica_total),
        moment_projection_input,
        squared_projection_input,
        factor_array,
        step_number,
    )
    state_out_b = adam_step(
        sum_out_b,
        local_portion(adapter_projection_output, common_index, replica_total * group_list),
        moment_projection_output,
        squared_projection_output,
        factor_array,
        step_number,
    )
    state_in_a = adam_step(
        summed_hidden_input,
        local_portion(adapter_hidden_input, replica_index, replica_total),
        moment_hidden_input,
        squared_hidden_input,
        factor_array,
        step_number,
    )
    state_mid_b = adam_step(
        sum_mid_b,
        local_portion(adapter_hidden_output, replica_index, replica_total),
        moment_hidden_output,
        squared_hidden_output,
        factor_array,
        step_number,
    )
    state_down_a = adam_step(
        sum_down_a,
        local_portion(adapter_down_input, replica_index, replica_total),
        moment_down_input,
        squared_down_input,
        factor_array,
        step_number,
    )
    state_down_b = adam_step(
        sum_down_b,
        local_portion(adapter_down_output, replica_index, replica_total),
        moment_down_output,
        squared_down_output,
        factor_array,
        step_number,
    )
    return (
        block_out.reshape(1, tok_dev, MODEL_WIDTH),
        grad_tokens.reshape(1, tok_dev, MODEL_WIDTH),
        norm_value.reshape(1),
        sum_qkv_a,
        state_qkv_a[0],
        state_qkv_a[1],
        state_qkv_a[2],
        sum_qkv_b,
        state_qkv_b[0],
        state_qkv_b[1],
        state_qkv_b[2],
        sum_out_a,
        state_out_a[0],
        state_out_a[1],
        state_out_a[2],
        sum_out_b,
        state_out_b[0],
        state_out_b[1],
        state_out_b[2],
        summed_hidden_input,
        state_in_a[0],
        state_in_a[1],
        state_in_a[2],
        sum_mid_b,
        state_mid_b[0],
        state_mid_b[1],
        state_mid_b[2],
        sum_down_a,
        state_down_a[0],
        state_down_a[1],
        state_down_a[2],
        sum_down_b,
        state_down_b[0],
        state_down_b[1],
        state_down_b[2],
    )


def solution(mesh):
    return jax.shard_map(
        per_device,
        mesh=mesh,
        in_specs=(
            P("dp", "expert", None),
            P("dp", "expert", None),
            P(),
            P(),
            P(None, None, "expert"),
            P("expert", None),
            P("expert", None, None, None),
            P("expert", None, None),
            P("dp", "expert", None),
            P("dp", "expert", None),
            P(),
            P(),
            P(),
            P(None, None, None, "expert"),
            P(None, None, "expert"),
            P(),
            P("expert", None, None, None, None),
            P("expert", None, None, None, None),
            P("expert", None, None, None),
            P("expert", None, None, None),
            P(None, None, None, ("dp", "expert")),
            P(None, None, None, ("expert", "dp")),
            P(None, None, ("expert", "dp")),
            P(None, None, ("dp", "expert")),
            P("expert", None, None, None, "dp"),
            P("expert", None, None, None, "dp"),
            P("expert", None, None, "dp"),
            P("expert", None, None, "dp"),
            P(None, None, None, ("dp", "expert")),
            P(None, None, None, ("expert", "dp")),
            P(None, None, ("expert", "dp")),
            P(None, None, ("dp", "expert")),
            P("expert", None, None, None, "dp"),
            P("expert", None, None, None, "dp"),
            P("expert", None, None, "dp"),
            P("expert", None, None, "dp"),
        ),
        out_specs=(
            P("dp", "expert", None),
            P("dp", "expert", None),
            P(),
            P(None, None, None, ("dp", "expert")),
            P(None, None, None, ("dp", "expert")),
            P(None, None, None, ("dp", "expert")),
            P(None, None, None, ("dp", "expert")),
            P(None, None, None, ("expert", "dp")),
            P(None, None, None, ("expert", "dp")),
            P(None, None, None, ("expert", "dp")),
            P(None, None, None, ("expert", "dp")),
            P(None, None, ("expert", "dp")),
            P(None, None, ("expert", "dp")),
            P(None, None, ("expert", "dp")),
            P(None, None, ("expert", "dp")),
            P(None, None, ("dp", "expert")),
            P(None, None, ("dp", "expert")),
            P(None, None, ("dp", "expert")),
            P(None, None, ("dp", "expert")),
            P("expert", None, None, None, "dp"),
            P("expert", None, None, None, "dp"),
            P("expert", None, None, None, "dp"),
            P("expert", None, None, None, "dp"),
            P("expert", None, None, None, "dp"),
            P("expert", None, None, None, "dp"),
            P("expert", None, None, None, "dp"),
            P("expert", None, None, None, "dp"),
            P("expert", None, None, "dp"),
            P("expert", None, None, "dp"),
            P("expert", None, None, "dp"),
            P("expert", None, None, "dp"),
            P("expert", None, None, "dp"),
            P("expert", None, None, "dp"),
            P("expert", None, None, "dp"),
            P("expert", None, None, "dp"),
        ),
        check_vma=False,
    )
```

profile of v0, /device:TPU:0, one launch (start us, length us, event | category | flops | bytes accessed | tf_op | source)
XLA Modules:
  0.0 1082.6 jit_solution(14924817037350381863)
XLA Ops:
  14.5 36.2 %all-gather.3.cloned.1.call-done = bf16[1024,2048]{1,0:T(8,128)(2,1)} async-done(((bf16[128,2048]{1,0:T(8,128)(2,1)}), bf16[1024,2048]{1,0:T(8,128)(2,1)}) %all-gather.3.cloned.1.call-update) | async-done | bytes 4194320 | tf_op jit(solution)/shard_map/all_gather | solution.py:123
  50.8 3.8 fusion.84
  56.6 3.5 fusion.74
  70.9 10.3 while.27
  82.5 2.7 fusion.112
  85.2 6.6 convolution_add_fusion
  92.9 4.5 reduce-window.6
  100.2 11.2 %scatter_custom_fusion.1 = bf16[1280,2048]{1,0:T(8,128)(2,1)} fusion(s32[1024]{0:T(1024)S(1)} %bitcast.326, f32[128,2048]{1,0:T(8,128)} %bitcast_convert_fusion, f32[1024]{0:T(1024)S(1)} %mul.645, bf16[]{:T(256)} %constant.70.clone.1), kind=kCustom, calls=%fused_computation.78 | custom fusion | flops 4194304 | bytes 6295554 | tf_op jit(solution)/shard_map/scatter | solution.py:223
  111.4 10.1 copy.171
  121.6 5.1 all-to-all-start.2
  126.8 74.5 %reduce-scatter.19.cloned.1.call-done = f32[128,2048]{1,0:T(8,128)} async-done(((f32[1024,2048]{1,0:T(8,128)}), f32[128,2048]{1,0:T(8,128)}) %reduce-scatter.19.cloned.1.call-update) | async-done | bytes 1048592 | tf_op jit(solution)/shard_map/reduce_scatter | solution.py:162
  205.2 24.8 %scatter_custom_fusion = bf16[1280,2048]{1,0:T(8,128)(2,1)} fusion(s32[1024]{0:T(1024)S(1)} %bitcast.327, bf16[128,2048]{1,0:T(8,128)(2,1)} %multiply_convert_fusion.6, s32[1024]{0:T(1024)S(1)} %broadcast_clamp_fusion.1, bf16[]{:T(256)} %constant.70.clone.1), kind=kCustom, calls=%fused_computation.85 | custom fusion | bytes 5243392 | tf_op jit(solution)/shard_map/scatter | solution.py:181
  230.0 10.2 copy.164
  240.2 9.6 all-to-all-start
  249.9 5.3 fusion.93
  255.2 15.3 %fusion.72 = f32[2,640,1024]{2,1,0:T(8,128)} fusion(bf16[2,1024,2048]{2,1,0:T(8,128)(2,1)} %param.47, bf16[2,640,2048]{2,0,1:T(2,128)(2,1)} %all-to-all-done.2), kind=kOutput, calls=%fused_computation.100 | convolution fusion | flops 5368709120 | bytes 18874368 | tf_op jit(solution)/shard_map/ecd,efd->ecf/dot_general | solution.py:235
  270.5 39.8 %all-to-all-done = bf16[2,640,2048]{2,0,1:T(2,128)(2,1)} async-done(((bf16[2,640,2048]{2,0,1:T(2,128)(2,1)}), bf16[2,640,2048]{2,0,1:T(2,128)(2,1)}, u32[]{:S(2)}, u32[]{:S(2)}) %all-to-all-start) | async-done | bytes 5242912 | tf_op jit(solution)/shard_map/all_to_all | solution.py:183
  310.3 5.5 fusion.87
  315.8 6.5 fusion.131
  322.3 24.1 %bitcast_add_fusion.1 = f32[2,2,640,1024]{3,2,1,0:T(8,128)} fusion(f32[2,2,640,1024]{3,2,1,0:T(8,128)} %fusion.131, bf16[2,2,2048,1024]{3,2,1,0:T(8,128)(2,1)} %param.46, bf16[2,640,2048,1]{2,0,1,3:T(2,128)(2,1)} %bitcast.22), kind=kOutput, calls=%fused_computation.51 | convolution fusion | flops 10740039680 | bytes 42991616 | tf_op jit(solution)/shard_map/ecd,ejdf->ejcf/dot_general | solution.py:197
  346.4 8.6 fusion.78
  357.4 2.4 fusion.90
  359.8 18.6 %fusion.33 = f32[2,640,2048,1]{2,1,0,3:T(8,128)} fusion(bf16[2,2,2048,1024]{3,2,1,0:T(8,128)(2,1)} %param.46, bf16[2,1,640,1024]{3,2,0,1:T(8,128)(2,1)} %copy-done.48, bf16[2,1,640,1024]{3,2,0,1:T(8,128)(2,1)} %copy-done.47), kind=kOutput, calls=%fused_computation.47 | convolution fusion | flops 10740039680 | bytes 32505856 | tf_op jit(solution)/shard_map/ejcf,ejdf->ecd/dot_general | solution.py:254
  378.4 8.0 fusion.35
  386.3 10.2 copy.176
  396.6 4.8 all-to-all-start.3
  401.4 2.7 convolution_convert_fusion
  404.1 8.0 fusion.194
  412.1 4.9 add_convert_fusion
  417.0 10.2 copy.168
  427.2 34.5 %all-to-all-done.3 = bf16[2,640,2048]{2,0,1:T(2,128)(2,1)} async-done(((bf16[2,640,2048]{2,0,1:T(2,128)(2,1)}), bf16[2,640,2048]{2,0,1:T(2,128)(2,1)}, u32[]{:S(2)}, u32[]{:S(2)}) %all-to-all-start.3) | async-done | bytes 5242912 | tf_op jit(solution)/shard_map/all_to_all | solution.py:263
  461.7 4.7 all-to-all-start.1
  466.6 7.3 copy.177
  473.9 12.2 %gather_fusion.1 = bf16[1024,2048]{1,0:T(8,128)(2,1)} fusion(bf16[1280,2048]{1,0:T(8,128)(2,1)} %bitcast.304, s32[1024]{0:T(1024)S(1)} %broadcast_clamp_fusion), kind=kCustom, calls=%fused_computation.2 | custom fusion | bytes 8392704 | tf_op jit(solution)/shard_map/gather | solution.py:267
  486.1 40.7 %all-to-all-done.1 = bf16[2,640,2048]{2,0,1:T(2,128)(2,1)} async-done(((bf16[2,640,2048]{2,0,1:T(2,128)(2,1)}), bf16[2,640,2048]{2,0,1:T(2,128)(2,1)}, u32[]{:S(2)}, u32[]{:S(2)}) %all-to-all-start.1) | async-done | bytes 5242912 | tf_op jit(solution)/shard_map/all_to_all | solution.py:212
  526.8 7.2 copy.169
  533.9 12.0 %gather_fusion = bf16[1024,2048]{1,0:T(8,128)(2,1)} fusion(bf16[1280,2048]{1,0:T(8,128)(2,1)} %bitcast.303, s32[1024]{0:T(1024)S(1)} %broadcast_clamp_fusion), kind=kCustom, calls=%fused_computation.1 | custom fusion | bytes 8392704 | tf_op jit(solution)/shard_map/gather | solution.py:216
  546.0 8.7 convert_reduce_fusion
  560.8 3.1 fusion.44
  565.6 5.3 fusion.68
  572.2 5.5 fusion.60
  579.9 13.0 %all-gather.5.cloned.1.call-done = bf16[1024,2048]{1,0:T(8,128)(2,1)} async-done(((bf16[128,2048]{1,0:T(8,128)(2,1)}), bf16[1024,2048]{1,0:T(8,128)(2,1)}) %all-gather.5.cloned.1.call-update) | async-done | bytes 4194320 | tf_op jit(solution)/shard_map/all_gather | solution.py:271
  592.9 3.5 fusion.143
  603.2 20.2 %while.28 = (s32[]{:T(128)}, f32[1024,2,128]{0,2,1:T(8,128)}, f32[1024,2,128]{0,2,1:T(8,128)}, bf16[2,512,2,128]{3,2,1,0:T(2,128)(2,1)}, bf16[2,512,2,128]{3,1,2...) while((s32[]{:T(128)}, f32[1024,2,128]{0,2,1:T(8,128)}, ...), condition=%wide.region_17.18_spmd.clone, body=%wide.region_15.17_spmd.clone.sunk | while | flops 1356332032 | bytes 66875788 | solution.py:309
  642.1 3.0 reshape.468
  645.4 3.9 fusion.196
  650.4 6.0 copy.209
  656.5 6.5 reshape.472
  670.2 14.8 %copy.203 = f32[3,8,16,2048]{2,1,0,3:T(8,128)} copy(f32[3,8,16,2048]{3,2,1,0:T(8,128)} %broadcast_multiply_fusion) | data formatting | bytes 6291456
  685.0 16.6 %reshape.466 = f32[2048,384]{1,0:T(8,128)} reshape(f32[2048,3,8,16]{3,2,1,0:T(8,128)} %bitcast.305) | data formatting | bytes 6291456
  701.9 4.8 fusion.181
  706.7 6.5 fusion.37
  716.3 2.4 multiply_reduce_fusion.6
  718.7 2.4 multiply_reduce_fusion.5
  721.1 2.8 multiply_reduce_fusion.2
  724.0 16.3 %reduce-scatter.35.cloned.1.call-done = bf16[64,128]{1,0:T(8,128)(2,1)} async-done(((bf16[256,128]{1,0:T(8,128)(2,1)}), bf16[64,128]{1,0:T(8,128)(2,1)}) %reduce-scatter.35.cloned.1.call-update) | async-done | bytes 16400
  742.5 18.4 %reduce-scatter.33.cloned.1.call-done = bf16[64,384]{1,0:T(8,128)(2,1)} async-done(((bf16[256,384]{1,0:T(8,128)(2,1)}), bf16[64,384]{1,0:T(8,128)(2,1)}) %reduce-scatter.33.cloned.1.call-update) | async-done | bytes 49168
  765.1 133.2 %reduce-scatter.37.cloned.1.call-done = f32[64,128]{1,0:T(8,128)} async-done(((f32[2048,128]{1,0:T(8,128)}), f32[64,128]{1,0:T(8,128)}) %reduce-scatter.37.cloned.1.call-update) | async-done | bytes 32784
  901.5 100.4 %reduce-scatter.31.cloned.1.call-done = f32[64,384]{1,0:T(8,128)} async-done(((f32[2048,384]{1,0:T(8,128)}), f32[64,384]{1,0:T(8,128)}) %reduce-scatter.31.cloned.1.call-update) | async-done | bytes 98320
  1011.1 40.1 %psum.7 = f32[]{:T(128)} all-reduce(f32[]{:T(128)S(6)} %add.379), channel_id=1, replica_groups=mesh['dp'=4,'expert'=8] {'dp','expert'}, use_global_device_ids=true, to_apply=%region_36.37 | all-reduce | flops 1 | bytes 8 | tf_op jit(solution)/shard_map/psum | solution.py:399
  1061.9 2.4 add_multiply_fusion.2
  1064.3 2.4 add_multiply_fusion.1
  1066.7 3.3 add_multiply_fusion
  1071.5 2.9 fusion.101
  (269 shorter events, 132.6 us)
Async XLA Ops:
  7.2 49.4 %copy-start = (bf16[3,2048,256]{2,1,0:T(8,128)(2,1)S(1)}, bf16[3,2048,256]{2,1,0:T(8,128)(2,1)}, u32[]{:S(2)}) copy-start(bf16[3,2048,256]{2,1,0:T(8,128)(2,1)} %param.44) | copy-start | bytes 9437188
  7.2 43.5 %all-gather.3.cloned.1.call-start = ((), (), s32[]{:S(2)}) async-start(), calls=%async_computation.14 | async-start | bytes 4718592 | tf_op jit(solution)/shard_map/all_gather | solution.py:123
  11.3 190.0 %reduce-scatter.19.cloned.1.call-start = ((), (), s32[]{:S(2)}) async-start(), calls=%async_computation.15 | async-start | bytes 9437184 | tf_op jit(solution)/shard_map/reduce_scatter | solution.py:162
  50.8 5.8 copy-start.3
  70.9 2.9 copy-start.12
  76.0 2.9 copy-start.12
  81.2 4.0 copy-start.39
  82.5 2.7 copy-start.34
  91.8 5.9 copy-start.41
  121.6 81.3 %copy-start.36 = (f32[2048]{0:T(1024)S(1)}, f32[2048]{0:T(1024)}, u32[]{:S(2)}) copy-start(f32[2048]{0:T(1024)} %param.43) | copy-start | bytes 24580
  121.6 118.7 %all-to-all-start.2 = ((bf16[2,640,2048]{2,0,1:T(2,128)(2,1)}), bf16[2,640,2048]{2,0,1:T(2,128)(2,1)}, u32[]{:S(2)}, u32[]{:S(2)}) async-start(bf16[2,640,2048]{2,0,1:T(2,128)(2,1)} %copy.171), calls=%async_computation.3 | async-start | bytes 10485760 | tf_op jit(solution)/shard_map/all_to_all | solution.py:225
  202.9 37.4 %copy-start.45 = (f32[128]{0:T(128)}, f32[128]{0:T(128)S(1)}, u32[]{:S(2)}) copy-start(f32[128]{0:T(128)S(1)} %add_rsqrt_fusion) | copy-start | bytes 1540
  240.2 70.1 %all-to-all-start = ((bf16[2,640,2048]{2,0,1:T(2,128)(2,1)}), bf16[2,640,2048]{2,0,1:T(2,128)(2,1)}, u32[]{:S(2)}, u32[]{:S(2)}) async-start(bf16[2,640,2048]{2,0,1:T(2,128)(2,1)} %copy.164), calls=%async_computation.1 | async-start | bytes 10485760 | tf_op jit(solution)/shard_map/all_to_all | solution.py:183
  355.1 1.5 copy-start.47
  355.1 2.4 copy-start.48
  396.6 65.2 %all-to-all-start.3 = ((bf16[2,640,2048]{2,0,1:T(2,128)(2,1)}), bf16[2,640,2048]{2,0,1:T(2,128)(2,1)}, u32[]{:S(2)}, u32[]{:S(2)}) async-start(bf16[2,640,2048]{2,0,1:T(2,128)(2,1)} %copy.176), calls=%async_computation.4 | async-start | bytes 10485760 | tf_op jit(solution)/shard_map/all_to_all | solution.py:263
  401.4 2.7 copy-start.2
  461.7 65.0 %all-to-all-start.1 = ((bf16[2,640,2048]{2,0,1:T(2,128)(2,1)}), bf16[2,640,2048]{2,0,1:T(2,128)(2,1)}, u32[]{:S(2)}, u32[]{:S(2)}) async-start(bf16[2,640,2048]{2,0,1:T(2,128)(2,1)} %copy.168), calls=%async_computation.2 | async-start | bytes 10485760 | tf_op jit(solution)/shard_map/all_to_all | solution.py:212
  466.4 126.5 %all-gather.5.cloned.1.call-start = ((), (), s32[]{:S(2)}) async-start(), calls=%async_computation.16 | async-start | bytes 4718592 | tf_op jit(solution)/shard_map/all_gather | solution.py:271
  545.9 8.7 copy-start.10
  545.9 8.7 copy-start.14
  545.9 8.7 copy-start.37
  545.9 9.1 copy-start.22
  545.9 9.1 copy-start.46
  556.9 157.1 %reduce-scatter.27.cloned.1.call-start = ((), (), s32[]{:S(2)}) async-start(), calls=%async_computation.20 | async-start | bytes 655360 | tf_op jit(solution)/shard_map/reduce_scatter | solution.py:374
  560.8 155.5 %reduce-scatter.25.cloned.1.call-start = ((), (), s32[]{:S(2)}) async-start(), calls=%async_computation.19 | async-start | bytes 1310720 | tf_op jit(solution)/shard_map/reduce_scatter | solution.py:368
  565.2 153.5 %reduce-scatter.29.cloned.1.call-start = ((), (), s32[]{:S(2)}) async-start(), calls=%async_computation.21 | async-start | bytes 1310720 | tf_op jit(solution)/shard_map/reduce_scatter | solution.py:380
  572.2 148.9 %reduce-scatter.23.cloned.1.call-start = ((), (), s32[]{:S(2)}) async-start(), calls=%async_computation.18 | async-start | bytes 2621440 | tf_op jit(solution)/shard_map/reduce_scatter | solution.py:362
  579.7 160.5 %reduce-scatter.35.cloned.1.call-start = ((), (), s32[]{:S(2)}) async-start(), calls=%async_computation.24 | async-start | bytes 81920
  592.9 3.5 copy-start.11
  592.9 3.8 copy-start.24
  596.7 6.5 copy-start.40
  603.2 3.1 copy-start.8
  606.2 1.3 copy-start.13
  607.5 1.3 copy-start.9
  608.9 1.9 copy-start.5
  608.9 1.9 copy-start.6
  610.0 1.4 copy-start.18
  613.3 3.1 copy-start.8
  616.3 1.3 copy-start.13
  617.6 1.3 copy-start.9
  619.0 1.9 copy-start.5
  619.0 1.9 copy-start.6
  620.2 1.4 copy-start.18
  623.4 15.2 %copy-start.33 = (bf16[3,16,1024]{2,1,0:T(8,128)(2,1)S(1)}, bf16[3,16,1024]{2,1,0:T(8,128)(2,1)}, u32[]{:S(2)}) copy-start(bf16[3,16,1024]{2,1,0:T(8,128)(2,1)} %copy-done.32) | copy-start | bytes 294916
  638.5 6.9 copy-start.35
  638.5 122.4 %reduce-scatter.33.cloned.1.call-start = ((), (), s32[]{:S(2)}) async-start(), calls=%async_computation.23 | async-start | bytes 245760
  645.1 253.2 %reduce-scatter.37.cloned.1.call-start = ((), (), s32[]{:S(2)}) async-start(), calls=%async_computation.25 | async-start | bytes 1081344
  663.0 338.9 %reduce-scatter.31.cloned.1.call-start = ((), (), s32[]{:S(2)}) async-start(), calls=%async_computation.22 | async-start | bytes 3244032
  663.0 2.7 copy-start.4
  701.6 368.4 %reduce-scatter.21.cloned.1.call-start = ((), (), s32[]{:S(2)}) async-start(), calls=%async_computation.17 | async-start | bytes 4718592 | tf_op jit(solution)/shard_map/reduce_scatter | solution.py:326
  900.0 157.6 %copy-start.27 = (f32[3,8,16,64]{3,2,1,0:T(8,128)S(1)}, f32[3,8,16,64]{3,2,1,0:T(8,128)}, u32[]{:S(2)}) copy-start(f32[3,8,16,64]{3,2,1,0:T(8,128)} %get-tuple-element.277) | copy-start | bytes 294916
  1005.3 59.0 %copy-start.23 = (f32[3,8,16,64]{3,2,1,0:T(8,128)}, f32[3,8,16,64]{3,2,1,0:T(8,128)S(1)}, u32[]{:S(2)}) copy-start(f32[3,8,16,64]{3,2,1,0:T(8,128)S(1)} %copy.204) | copy-start | bytes 294916
  1052.0 9.9 copy-start.20
  1052.0 9.9 copy-start.28
  1052.0 9.9 copy-start.29
  1052.0 12.3 %copy-start.21 = (f32[2,8,16,512]{3,2,1,0:T(8,128)S(1)}, f32[2,8,16,512]{3,2,1,0:T(8,128)}, u32[]{:S(2)}) copy-start(f32[2,8,16,512]{3,2,1,0:T(8,128)} %get-tuple-element.267) | copy-start | bytes 1572868
  1052.0 12.3 %copy-start.30 = (f32[2,8,16,512]{3,2,1,0:T(8,128)S(1)}, f32[2,8,16,512]{3,2,1,0:T(8,128)}, u32[]{:S(2)}) copy-start(f32[2,8,16,512]{3,2,1,0:T(8,128)} %param.75) | copy-start | bytes 1572868
  1052.0 12.3 %copy-start.31 = (f32[2,8,16,512]{3,2,1,0:T(8,128)S(1)}, f32[2,8,16,512]{3,2,1,0:T(8,128)}, u32[]{:S(2)}) copy-start(f32[2,8,16,512]{3,2,1,0:T(8,128)} %param.67) | copy-start | bytes 1572868
  1059.6 7.1 copy-start.17
  1059.6 7.1 copy-start.25
  1059.6 7.1 copy-start.26
  1066.7 3.3 copy-start.38
  1066.7 4.8 copy-start.44
  (13 other events, 11.7 us)
Sparse Core Ops, SparseCore 0:
  11.4 39.2 all-gather.2
  91.9 109.2 reduce-scatter.18
  557.0 35.8 all-gather.4
  595.6 21.8 reduce-scatter.26
  620.3 25.5 reduce-scatter.24
  648.6 25.7 reduce-scatter.28
  676.8 42.1 reduce-scatter.22
  721.7 18.4 reduce-scatter.34
  743.1 17.7 reduce-scatter.32
  763.6 134.7 reduce-scatter.36
  903.7 98.0 reduce-scatter.30
  1005.1 50.5 reduce-scatter.20
where the time goes:
time: 1090 us; the launch traced here: 1080 us
  waiting for transfers between devices  507 us (47%)
  local copies, waits for them, and re-layouts  200 us (18%)
  matrix products  193 us (18%)
  other arithmetic  91.8 us (8%)
  blocking collectives  40.1 us (4%)
  starting transfers between devices  25.7 us (2%)
  between operations  24.9 us (2%)
    unnamed x16, waiting for transfers between devices  268 us
    reduce_scatter x1, waiting for transfers between devices, per_device(): lax.psum_scatter(jnp.dot(mixed, output_weight, preferred_element_type=sin...  74.5 us
    unnamed x92, local copies, waits for them, and re-layouts  65.3 us
    all_to_all x1, waiting for transfers between devices, per_device(): lax.all_to_all(expert_out, 'expert', split_axis=1, concat_axis=1, tiled=T...  40.7 us
    psum x1, blocking collectives, per_device(): norm_value = jnp.sqrt(lax.psum(squares, ('dp', 'expert')))  40.1 us
    all_to_all x1, waiting for transfers between devices, per_device(): lax.all_to_all(outgoing.reshape(EXP_DEV, group_list * cap, MODEL_WIDTH),...  39.8 us
    all_gather x1, waiting for transfers between devices, per_device(): sequence = lax.all_gather(normed, 'expert', axis=0, tiled=True)  36.2 us
    all_to_all x1, waiting for transfers between devices, per_device(): lax.all_to_all(grad_slots, 'expert', split_axis=1, concat_axis=1, tiled=T...  34.5 us
  transfers between devices with their start and end apart: 16, of which 10 were waited for; matrix products, arithmetic and copies ran while one was open for 29% of the time, Pallas kernels for 0%

commit v1 on v0

--- a/solution.py
+++ b/solution.py
@@ -118,190 +118,141 @@
     cap = min(tok_dev, tok_dev * TOP * 5 // (4 * experts_all))
     picked_projection_input = select_adapter(adapter_projection_input, adapter_slot, 0)
     picked_projection_output = select_adapter(adapter_projection_output, adapter_slot, 0)
+    picked_attention_input = select_adapter(adapter_attention_input, adapter_slot, 1)
+    picked_attention_output = select_adapter(adapter_attention_output, adapter_slot, 1)
+    picked_hidden_input = select_adapter(adapter_hidden_input, adapter_slot, 2)
+    picked_hidden_output = select_adapter(adapter_hidden_output, adapter_slot, 2)
+    picked_down_input = select_adapter(adapter_down_input, adapter_slot, 1)
+    picked_down_output = select_adapter(adapter_down_output, adapter_slot, 1)
+
+    def mm(spec, left, right):
+        return jnp.einsum(spec, left, right, preferred_element_type=single)
+
     tokens = hidden[0].astype(single)
     normed = rms_scale(tokens, attention_gain).astype(brain)
     sequence = lax.all_gather(normed, "expert", axis=0, tiled=True)
-    picked_attention_input = select_adapter(adapter_attention_input, adapter_slot, 1)
-    picked_attention_output = select_adapter(adapter_attention_output, adapter_slot, 1)
-    low_qkv = jnp.einsum(
-        "ld,jrd->jlr", sequence, picked_attention_input, preferred_element_type=single
+    top_seq = lax.all_gather(output_cotangent[0], "expert", axis=0, tiled=True)
+    routes = token_experts[0]
+    dense = jnp.sum(
+        jnp.where(
+            routes[:, :, None] == jnp.arange(experts_all, dtype=jnp.int32)[None, None, :],
+            expert_gate_weight[0][:, :, None],
+            0.0,
+        ),
+        axis=1,
+    )
+    dense_all = lax.all_gather(dense.T, "expert", axis=0, tiled=False)
+    dense_here = lax.dynamic_slice_in_dim(dense_all, group_index * EXP_DEV, EXP_DEV, 1)
+    chosen = dense_here > 0.0
+    upper = (
+        jnp.arange(tok_dev)[:, None] < jnp.arange(tok_dev)[None, :]
     ).astype(brain)
-    project = jnp.einsum(
-        "ld,jde->jle", sequence, query_key_value_weight, preferred_element_type=single
-    )
-    project = (
-        project
-        + jnp.einsum(
-            "jlr,jre->jle", low_qkv, picked_attention_output, preferred_element_type=single
-        )
+    place = mm("bet,tu->beu", chosen.astype(brain), upper).astype(jnp.int32)
+    pick = (
+        (place[:, :, None, :] == jnp.arange(cap, dtype=jnp.int32)[None, None, :, None])
+        & chosen[:, :, None, :]
     ).astype(brain)
+    slot_weight = jnp.sum(pick.astype(single) * dense_here[:, :, None, :], axis=-1)
+    slot_weight = jnp.transpose(slot_weight, (1, 0, 2)).reshape(EXP_DEV, group_list * cap, 1)
+
+    low_qkv = mm("ld,jrd->jlr", sequence, picked_attention_input).astype(brain)
+    project = mm("ld,jde->jle", sequence, query_key_value_weight)
+    project = (project + mm("jlr,jre->jle", low_qkv, picked_attention_output)).astype(brain)
     queries = project[0].reshape(length, heads_here, HEAD)
     keys = project[1].reshape(length, heads_here, HEAD)
     values = project[2].reshape(length, heads_here, HEAD)
 
     def attend(query_block):
-        scores = (
-            jnp.einsum("bhd,khd->hbk", query_block, keys, preferred_element_type=single) * scale
-        )
+        scores = mm("bhd,khd->hbk", query_block, keys) * scale
         peak = jnp.max(scores, axis=-1, keepdims=True)
         expo = jnp.exp(scores - peak)
         totals = jnp.sum(expo, axis=-1, keepdims=True)
         probs = (expo / totals).astype(brain)
-        mixed_block = jnp.einsum(
-            "hbk,khd->bhd", probs, values, preferred_element_type=single
-        ).astype(brain)
+        mixed_block = mm("hbk,khd->bhd", probs, values).astype(brain)
         return (mixed_block, (peak + jnp.log(totals))[..., 0])
 
     query_blocks = queries.reshape(nblocks, block, heads_here, HEAD)
     mixed, log_sums = lax.map(attend, query_blocks)
     mixed = mixed.reshape(length, width_here)
-    out_rank = jnp.einsum(
-        "le,re->lr", mixed, picked_projection_input, preferred_element_type=single
-    )
-    ranks = out_rank
+    out_rank = mm("le,re->lr", mixed, picked_projection_input).astype(brain)
     branch = lax.psum_scatter(
-        jnp.dot(mixed, output_weight, preferred_element_type=single)
-        + jnp.dot(ranks, picked_projection_output.astype(single), precision=highest),
+        (jnp.dot(mixed, output_weight, preferred_element_type=single)
+        + jnp.dot(out_rank, picked_projection_output, preferred_element_type=single)).astype(brain),
         "expert",
         scatter_dimension=0,
         tiled=True,
-    )
+    ).astype(single)
     resid = tokens + branch
     moe_in = rms_scale(resid, expert_norm_gain).astype(brain)
-    routes = token_experts[0].reshape(-1)
-    onehot = (routes[:, None] == jnp.arange(experts_all, dtype=jnp.int32)[None, :]).astype(
-        jnp.int32
-    )
-    within = jnp.sum((jnp.cumsum(onehot, axis=0) - 1) * onehot, axis=1)
-    slots = routes % EXP_DEV * (group_list * cap) + routes // EXP_DEV * cap + within
-    token_rows = jnp.repeat(jnp.arange(tok_dev, dtype=jnp.int32), TOP)
-    outgoing = (
-        jnp.zeros((EXP_DEV * group_list * cap, MODEL_WIDTH), brain)
-        .at[slots]
-        .set(moe_in[token_rows])
-    )
-    arrived = lax.all_to_all(
-        outgoing.reshape(EXP_DEV, group_list * cap, MODEL_WIDTH),
-        "expert",
-        split_axis=1,
-        concat_axis=1,
-        tiled=True,
-    )
-    picked_hidden_input = select_adapter(adapter_hidden_input, adapter_slot, 2)
-    picked_hidden_output = select_adapter(adapter_hidden_output, adapter_slot, 2)
-    picked_down_input = select_adapter(adapter_down_input, adapter_slot, 1)
-    picked_down_output = select_adapter(adapter_down_output, adapter_slot, 1)
-    in_rank = jnp.einsum(
-        "ecd,ejrd->ejcr", arrived, picked_hidden_input, preferred_element_type=single
-    ).astype(brain)
-    gate_up = jnp.einsum("ecd,ejdf->ejcf", arrived, gate_up_weight, preferred_element_type=single)
-    gate_up = gate_up + jnp.einsum(
-        "ejcr,ejrf->ejcf", in_rank, picked_hidden_output, preferred_element_type=single
-    )
+    moe_seq = lax.all_gather(moe_in, "expert", axis=0, tiled=True)
+
+    def gather_rows(seq):
+        rows = mm("best,btd->ebsd", pick, seq.reshape(group_list, tok_dev, -1)).astype(brain)
+        return rows.reshape(EXP_DEV, group_list * cap, -1)
+
+    def combine(rows):
+        rows = rows.reshape(EXP_DEV, group_list, cap, -1)
+        return mm("best,ebsd->btd", pick, rows).reshape(length, -1)
+
+    top_rows = gather_rows(top_seq)
+    arrived = gather_rows(moe_seq)
+    in_rank = mm("ecd,ejrd->ejcr", arrived, picked_hidden_input).astype(brain)
+    gate_up = mm("ecd,ejdf->ejcf", arrived, gate_up_weight)
+    gate_up = gate_up + mm("ejcr,ejrf->ejcf", in_rank, picked_hidden_output)
     sigmoid_gate = jax.nn.sigmoid(gate_up[:, 0])
     swish_gate = gate_up[:, 0] * sigmoid_gate
     active = (swish_gate * gate_up[:, 1]).astype(brain)
-    down_rank = jnp.einsum(
-        "ecf,erf->ecr", active, picked_down_input, preferred_element_type=single
-    ).astype(brain)
-    expert_out = jnp.einsum("ecf,efd->ecd", active, down_weight, preferred_element_type=single)
-    expert_out = (
-        expert_out
-        + jnp.einsum("ecr,erd->ecd", down_rank, picked_down_output, preferred_element_type=single)
-    ).astype(brain)
-    returned = lax.all_to_all(
-        expert_out, "expert", split_axis=1, concat_axis=1, tiled=True
-    ).reshape(-1, MODEL_WIDTH)
-    route_weight = expert_gate_weight[0]
-    picked = returned[slots].reshape(tok_dev, TOP, MODEL_WIDTH).astype(single)
-    block_out = (resid + jnp.sum(route_weight[:, :, None] * picked, axis=1)).astype(brain)
+    down_rank = mm("ecf,erf->ecr", active, picked_down_input).astype(brain)
+    expert_out = mm("ecf,efd->ecd", active, down_weight)
+    expert_out = expert_out + mm("ecr,erd->ecd", down_rank, picked_down_output)
+    expert_out = (slot_weight * expert_out).astype(brain)
+    moe_out = lax.psum_scatter(
+        combine(expert_out).astype(brain), "expert", scatter_dimension=0, tiled=True
+    ).astype(single)
+    block_out = (resid + moe_out).astype(brain)
     grad_top = output_cotangent[0].astype(single)
-    grad_copies = (
-        (route_weight[:, :, None] * grad_top[:, None, :]).astype(brain).reshape(-1, MODEL_WIDTH)
-    )
-    outgoing_grad = (
-        jnp.zeros((EXP_DEV * group_list * cap, MODEL_WIDTH), brain).at[slots].set(grad_copies)
-    )
-    grad_expert = lax.all_to_all(
-        outgoing_grad.reshape(EXP_DEV, group_list * cap, MODEL_WIDTH),
-        "expert",
-        split_axis=1,
-        concat_axis=1,
-        tiled=True,
-    )
-    grad_down_rank = jnp.einsum(
-        "ecd,erd->ecr", grad_expert, picked_down_output, preferred_element_type=single
-    ).astype(brain)
-    grad_active = jnp.einsum(
-        "ecd,efd->ecf", grad_expert, down_weight, preferred_element_type=single
-    )
-    grad_active = grad_active + jnp.einsum(
-        "ecr,erf->ecf", grad_down_rank, picked_down_input, preferred_element_type=single
-    )
-    grad_active = grad_active.astype(brain).astype(single)
-    g_down_b = jnp.einsum("ecr,ecd->erd", down_rank, grad_expert, preferred_element_type=single)
-    g_down_a = jnp.einsum("ecr,ecf->erf", grad_down_rank, active, preferred_element_type=single)
+    grad_down_rank = (slot_weight * mm("ecd,erd->ecr", top_rows, picked_down_output)).astype(brain)
+    grad_active = slot_weight * mm("ecd,efd->ecf", top_rows, down_weight)
+    grad_active = grad_active + mm("ecr,erf->ecf", grad_down_rank, picked_down_input)
+    g_down_b = mm("ecr,ecd->erd", (slot_weight * down_rank).astype(brain), top_rows)
+    g_down_a = mm("ecr,ecf->erf", grad_down_rank, active)
     grad_gate = (
         grad_active * gate_up[:, 1] * sigmoid_gate * (1.0 + gate_up[:, 0] * (1.0 - sigmoid_gate))
     )
     grad_up = grad_active * swish_gate
     grad_gate_up = jnp.stack([grad_gate, grad_up], axis=1).astype(brain)
-    grad_in_rank = jnp.einsum(
-        "ejcf,ejrf->ejcr", grad_gate_up, picked_hidden_output, preferred_element_type=single
-    ).astype(brain)
-    g_mid_b = jnp.einsum("ejcr,ejcf->ejrf", in_rank, grad_gate_up, preferred_element_type=single)
-    g_in_a = jnp.einsum("ejcr,ecd->ejrd", grad_in_rank, arrived, preferred_element_type=single)
-    grad_slots = jnp.einsum(
-        "ejcf,ejdf->ecd", grad_gate_up, gate_up_weight, preferred_element_type=single
-    )
-    grad_slots = (
-        grad_slots
-        + jnp.einsum(
-            "ejcr,ejrd->ecd", grad_in_rank, picked_hidden_input, preferred_element_type=single
-        )
-    ).astype(brain)
-    came_back = lax.all_to_all(
-        grad_slots, "expert", split_axis=1, concat_axis=1, tiled=True
-    ).reshape(-1, MODEL_WIDTH)
-    grad_moe_in = jnp.sum(
-        came_back[slots].reshape(tok_dev, TOP, MODEL_WIDTH).astype(single), axis=1
-    )
+    grad_in_rank = mm("ejcf,ejrf->ejcr", grad_gate_up, picked_hidden_output).astype(brain)
+    g_mid_b = mm("ejcr,ejcf->ejrf", in_rank, grad_gate_up)
+    g_in_a = mm("ejcr,ecd->ejrd", grad_in_rank, arrived)
+    grad_slots = mm("ejcf,ejdf->ecd", grad_gate_up, gate_up_weight)
+    grad_slots = (grad_slots + mm("ejcr,ejrd->ecd", grad_in_rank, picked_hidden_input)).astype(brain)
+    grad_moe_in = lax.psum_scatter(
+        combine(grad_slots).astype(brain), "expert", scatter_dimension=0, tiled=True
+    ).astype(single)
     grad_resid = grad_top + norm_back(resid, expert_norm_gain, grad_moe_in)
     grad_branch = grad_resid.astype(brain)
     branch_full = lax.all_gather(grad_branch, "expert", axis=0, tiled=True)
-    grad_out_rank = jnp.einsum(
-        "ld,rd->lr", branch_full, picked_projection_output, preferred_element_type=single
-    )
-    grad_mixed = jnp.einsum("ld,ed->le", branch_full, output_weight, preferred_element_type=single)
+    grad_out_rank = mm("ld,rd->lr", branch_full, picked_projection_output).astype(brain)
+    grad_mixed = mm("ld,ed->le", branch_full, output_weight)
     grad_mixed = (
         grad_mixed
-        + jnp.dot(grad_out_rank, picked_projection_input.astype(single), precision=highest)
+        + jnp.dot(grad_out_rank, picked_projection_input, preferred_element_type=single)
     ).astype(brain)
-    g_out_b = jnp.einsum("lr,ld->rd", out_rank, branch_full.astype(single), precision=highest)
-    g_out_a = jnp.einsum("lr,le->re", grad_out_rank, mixed.astype(single), precision=highest)
+    g_out_b = mm("lr,ld->rd", out_rank, branch_full)
+    g_out_a = mm("lr,le->re", grad_out_rank, mixed)
 
     def back_block(carry, items):
         grad_keys, grad_values = carry
         query_block, grad_block, log_block = items
-        scores = (
-            jnp.einsum("bhd,khd->hbk", query_block, keys, preferred_element_type=single) * scale
-        )
+        scores = mm("bhd,khd->hbk", query_block, keys) * scale
         probs = jnp.exp(scores - log_block[..., None])
-        grad_probs = jnp.einsum("bhd,khd->hbk", grad_block, values, preferred_element_type=single)
+        grad_probs = mm("bhd,khd->hbk", grad_block, values)
         grad_scores = (
             probs * (grad_probs - jnp.sum(grad_probs * probs, axis=-1, keepdims=True))
         ).astype(brain)
-        grad_query = (
-            jnp.einsum("hbk,khd->bhd", grad_scores, keys, preferred_element_type=single) * scale
-        )
-        grad_keys = (
-            grad_keys
-            + jnp.einsum("hbk,bhd->khd", grad_scores, query_block, preferred_element_type=single)
-            * scale
-        )
-        grad_values = grad_values + jnp.einsum(
-            "hbk,bhd->khd", probs.astype(brain), grad_block, preferred_element_type=single
-        )
+        grad_query = mm("hbk,khd->bhd", grad_scores, keys) * scale
+        grad_keys = grad_keys + mm("hbk,bhd->khd", grad_scores, query_block) * scale
+        grad_values = grad_values + mm("hbk,bhd->khd", probs.astype(brain), grad_block)
         return ((grad_keys, grad_values), grad_query.astype(brain))
 
     zeros_heads = jnp.zeros((length, heads_here, HEAD), single)
@@ -317,73 +268,66 @@
         ],
         axis=0,
     )
-    g_qkv_b = jnp.einsum("jlr,jle->jre", low_qkv, grad_project, preferred_element_type=single)
-    grad_low = jnp.einsum(
-        "jle,jre->jlr", grad_project, picked_attention_output, preferred_element_type=single
-    )
-    g_qkv_a = jnp.einsum("jlr,ld->jrd", grad_low, sequence.astype(single), precision=highest)
-    ranks = grad_low
+    g_qkv_b = mm("jlr,jle->jre", low_qkv, grad_project)
+    grad_low = mm("jle,jre->jlr", grad_project, picked_attention_output).astype(brain)
+    g_qkv_a = mm("jlr,ld->jrd", grad_low, sequence)
     grad_normed = lax.psum_scatter(
         (
-            jnp.einsum(
-                "jle,jde->ld", grad_project, query_key_value_weight, preferred_element_type=single
-            )
-            + jnp.einsum(
-                "jlr,jrd->ld", ranks, picked_attention_input.astype(single), precision=highest
-            )
+            mm("jle,jde->ld", grad_project, query_key_value_weight)
+            + mm("jlr,jrd->ld", grad_low, picked_attention_input)
         ).astype(jnp.bfloat16),
         "expert",
         scatter_dimension=0,
         tiled=True,
     ).astype(jnp.float32)
     grad_tokens = grad_resid + norm_back(tokens, attention_gain, grad_normed)
-    marker = (jnp.arange(ADAPTER_COUNT, dtype=jnp.int32) == adapter_slot).astype(single)
-    sum_qkv_a, sum_out_b = (
-        lax.psum_scatter(
-            spread_out(g_qkv_a, marker, 1), ("dp", "expert"), scatter_dimension=3, tiled=True
-        ),
-        lax.psum_scatter(
-            spread_out(g_out_b, marker, 0), ("dp", "expert"), scatter_dimension=2, tiled=True
-        ),
-    )
-    sum_qkv_b, sum_out_a, summed_hidden_input, sum_mid_b, sum_down_a, sum_down_b = (
-        lax.psum_scatter(
-            spread_out(g_qkv_b, marker, 1).astype(jnp.bfloat16),
-            "dp",
-            scatter_dimension=3,
-            tiled=True,
-        ).astype(jnp.float32),
-        lax.psum_scatter(
-            spread_out(g_out_a, marker, 0).astype(jnp.bfloat16),
-            "dp",
-            scatter_dimension=2,
-            tiled=True,
-        ).astype(jnp.float32),
-        lax.psum_scatter(
-            spread_out(g_in_a, marker, 2).astype(jnp.bfloat16),
-            "dp",
-            scatter_dimension=4,
-            tiled=True,
-        ).astype(jnp.float32),
-        lax.psum_scatter(
-            spread_out(g_mid_b, marker, 2).astype(jnp.bfloat16),
-            "dp",
-            scatter_dimension=4,
-            tiled=True,
-        ).astype(jnp.float32),
-        lax.psum_scatter(
-            spread_out(g_down_a, marker, 1).astype(jnp.bfloat16),
-            "dp",
-            scatter_dimension=3,
-            tiled=True,
-        ).astype(jnp.float32),
-        lax.psum_scatter(
-            spread_out(g_down_b, marker, 1).astype(jnp.bfloat16),
-            "dp",
-            scatter_dimension=3,
-            tiled=True,
-        ).astype(jnp.float32),
-    )
+
+    rank = g_out_b.shape[0]
+    chosen_adapters = (
+        sequence_adapter[:, None] == jnp.arange(ADAPTER_COUNT, dtype=jnp.int32)[None, :]
+    ).astype(single)
+
+    def columns(grad):
+        return jnp.moveaxis(
+            grad.reshape(-1, replica_total, grad.shape[-1] // replica_total), 1, 0
+        )
+
+    def place_adapters(pieces, shape):
+        spread = jnp.sum(
+            pieces[:, :, None] * chosen_adapters[:, None, :, None, None], axis=0
+        )
+        return spread.reshape(shape)
+
+    per_expert = [g_in_a, g_mid_b, g_down_a, g_down_b, g_qkv_b, g_out_a]
+    split = [columns(grad.astype(brain)) for grad in per_expert]
+    flat = [part.reshape(replica_total, -1, rank * part.shape[-1]) for part in split]
+    joined = jnp.concatenate([part.reshape(replica_total, -1) for part in flat], axis=1)
+    swapped = lax.all_to_all(
+        joined.reshape(replica_total, -1, 128), "dp", split_axis=0, concat_axis=0, tiled=True
+    ).reshape(replica_total, -1)
+    at = 0
+    placed = []
+    for grad, part in zip(per_expert, split):
+        size = part.shape[1] * part.shape[2]
+        got = swapped[:, at : at + size].astype(single)
+        at = at + size
+        lead = grad.shape[:-2]
+        got = got.reshape(replica_total, -1, rank, part.shape[2])
+        placed.append(place_adapters(got, lead + (ADAPTER_COUNT, rank, part.shape[2])))
+    summed_hidden_input, sum_mid_b, sum_down_a, sum_down_b, sum_qkv_b, sum_out_a = placed
+
+    shared = jnp.concatenate([g_qkv_a.reshape(-1, MODEL_WIDTH), g_out_b], axis=0)
+    piece = MODEL_WIDTH // (replica_total * group_list)
+    shared = jnp.transpose(
+        shared.reshape(-1, replica_total, group_list, piece), (2, 0, 1, 3)
+    ).reshape(group_list, -1, replica_total * piece)
+    shared = lax.psum_scatter(shared, "expert", scatter_dimension=0, tiled=True)[0]
+    shared = jnp.moveaxis(shared.reshape(-1, replica_total, piece), 1, 0)
+    shared = lax.all_to_all(shared, "dp", split_axis=0, concat_axis=0, tiled=True)
+    shared = shared.reshape(replica_total, -1, rank, piece)
+    shared = place_adapters(shared, (-1, ADAPTER_COUNT, rank, piece))
+    sum_qkv_a, sum_out_b = shared[:3], shared[3]
+
     squares = jnp.zeros((), single)
     for grad in (
         sum_qkv_a,

time: 1090 us -> 617 us (0.57)
  waiting for transfers between devices: 507 us -> 212 us
  local copies, waits for them, and re-layouts: 200 us -> 63.1 us
  other arithmetic: 91.8 us -> 57 us
  starting transfers between devices: 25.7 us -> 9.57 us
    unnamed x16 -> x9, waiting for transfers between devices: 268 us -> 0.81 us
    all_to_all x4 -> x2, waiting for transfers between devices: 115 us -> 7.77 us  [the longest x1 4.61 us: per_device(): lax.all_to_all(joined.reshape(replica_total, -1, 128), 'dp', split_axis=0...]
    all_gather x0 -> x2, waiting for transfers between devices: none -> 50.4 us  [the longest x1 25.6 us: per_device(): moe_seq = lax.all_gather(moe_in, 'expert', axis=0, tiled=True)]
    unnamed x92 -> x121, local copies, waits for them, and re-layouts: 65.3 us -> 20.6 us
    reduce_scatter x6 -> x5, waiting for transfers between devices: 74.5 us -> 113 us  [the longest x1 51.2 us: per_device(): lax.psum_scatter(combine(grad_slots).astype(brain), 'expert', scatter_dim...]
    scatter x1 -> x0, local copies, waits for them, and re-layouts: 24.8 us -> none  [per_device(): outgoing = jnp.zeros((EXP_DEV * group_list * cap, MODEL_WIDTH), brain).at...]
    gather x2 -> x0, local copies, waits for them, and re-layouts: 24.2 us -> none  [the longest x1 12.2 us: per_device(): came_back[slots].reshape(tok_dev, TOP, MODEL_WIDTH).astype(single)]
    convert_element_type x2 -> x3, local copies, waits for them, and re-layouts: 20.4 us -> 1.3 us  [the longest x2 1.29 us: gather_rows(): mm('best,btd->ebsd', pick, seq.reshape(group_list, tok_dev, -1))]
  transfers between devices with their start and end apart: 16 -> 11, of which waited for: 10 -> 9; matrix products, arithmetic and copies ran while one was open for 29% -> 19% of each run, Pallas kernels for 0% -> 0%
where the time goes in v1:
time: 617 us; the launch traced here: 605 us
  waiting for transfers between devices  212 us (34%)
  matrix products  192 us (31%)
  local copies, waits for them, and re-layouts  63.1 us (10%)
  other arithmetic  57 us (9%)
  blocking collectives  46.6 us (8%)
  between operations  24.9 us (4%)
  starting transfers between devices  9.57 us (2%)
    dot_general x48, matrix products, mm(): return jnp.einsum(spec, left, right, preferred_element_type=single)  183 us
    reduce_scatter x1, waiting for transfers between devices, per_device(): lax.psum_scatter(combine(grad_slots).astype(brain), 'expert', scatter_dim...  51.2 us
    reduce_scatter x1, waiting for transfers between devices, per_device(): lax.psum_scatter((jnp.dot(mixed, output_weight, preferred_element_type=si...  50.3 us
    psum x1, blocking collectives, per_device(): norm_value = jnp.sqrt(lax.psum(squares, ('dp', 'expert')))  37.4 us
    all_gather x1, waiting for transfers between devices, per_device(): sequence = lax.all_gather(normed, 'expert', axis=0, tiled=True)  36.2 us
    all_gather x1, waiting for transfers between devices, per_device(): moe_seq = lax.all_gather(moe_in, 'expert', axis=0, tiled=True)  25.6 us
    all_gather x1, waiting for transfers between devices, per_device(): top_seq = lax.all_gather(output_cotangent[0], 'expert', axis=0, tiled=True)  24.8 us
    unnamed x121, local copies, waits for them, and re-layouts  20.6 us
  transfers between devices with their start and end apart: 11, of which 9 were waited for; matrix products, arithmetic and copies ran while one was open for 19% of the time, Pallas kernels for 0%

profile of v1, /device:TPU:0, one launch (start us, length us, event | category | flops | bytes accessed | tf_op | source)
XLA Modules:
  0.0 605.3 jit_solution(1250373153313155974)
XLA Ops:
  9.2 2.0 fusion.74
  14.5 36.2 %all-gather.7.cloned.1.call-done = bf16[1024,2048]{1,0:T(8,128)(2,1)} async-done(((bf16[128,2048]{1,0:T(8,128)(2,1)}), bf16[1024,2048]{1,0:T(8,128)(2,1)}) %all-gather.7.cloned.1.call-update) | async-done | bytes 4194320 | tf_op jit(solution)/shard_map/all_gather | solution.py:133
  50.7 3.8 fusion.67
  56.5 3.5 fusion.56
  61.2 2.0 copy.201
  63.2 2.0 copy.200
  65.2 2.2 reshape_reshape_squeeze.3
  70.5 10.3 %while.27 = (s32[]{:T(128)}, bf16[2,512,2,128]{3,2,1,0:T(2,128)(2,1)}, f32[2,2,512]{2,1,0:T(2,128)S(1)}, bf16[2,512,2,128]{3,1,2,0:T(8,128)(2,1)}, bf16[1024,2,1...) while((s32[]{:T(128)}, bf16[2,512,2,128]{3,2,1,0:T(2,128)(2,1)}, ...), condition=%wide.region_4.5_spmd, body=%wide.region_1.4_spmd.sunk | while | flops 546438144 | bytes 21004468 | solution.py:175
  82.1 2.7 fusion.94
  84.8 4.1 add_convert_fusion
  89.9 50.3 %reduce-scatter.6.cloned.1.call-done = bf16[128,2048]{1,0:T(8,128)(2,1)} async-done(((bf16[1024,2048]{1,0:T(8,128)(2,1)}), bf16[128,2048]{1,0:T(8,128)(2,1)}) %reduce-scatter.6.cloned.1.call-update) | async-done | bytes 524304 | tf_op jit(solution)/shard_map/reduce_scatter | solution.py:178
  141.7 2.2 multiply_convert_fusion.5
  144.0 9.2 %all-gather = f32[128,128]{1,0:T(8,128)S(1)} all-gather(f32[16,128]{1,0:T(8,128)S(1)} %bitcast.395), channel_id=2, replica_groups=mesh['dp'=4,'expert'=8] {'expert'}, dimensions={0}, use_global_device_ids=true | all-gather | bytes 73728 | tf_op jit(solution)/shard_map/all_gather | solution.py:144
  153.9 24.8 %all-gather.13.cloned.1.call-done = bf16[1,1024,2048]{2,1,0:T(8,128)(2,1)} async-done(((bf16[1,128,2048]{2,1,0:T(8,128)(2,1)}), bf16[1,1024,2048]{2,1,0:T(8,128)(2,1)}) %all-gather.13.cloned.1.call-update) | async-done | bytes 4194320 | tf_op jit(solution)/shard_map/all_gather | solution.py:134
  178.8 3.7 convert_bitcast_fusion
  183.3 2.4 copy-done.2
  185.7 2.4 fusion.73
  188.0 4.1 fusion.128
  192.1 25.6 %all-gather.9.cloned.1.call-done = bf16[1024,2048]{1,0:T(8,128)(2,1)} async-done(((bf16[128,2048]{1,0:T(8,128)(2,1)}), bf16[1024,2048]{1,0:T(8,128)(2,1)}) %all-gather.9.cloned.1.call-update) | async-done | bytes 4194320 | tf_op jit(solution)/shard_map/all_gather | solution.py:187
  217.7 3.7 convert_bitcast_fusion.1
  221.8 2.8 convolution_convert_fusion.3
  224.7 17.2 %fusion.177 = f32[2,640,2,1024]{3,1,2,0:T(8,128)} fusion(bf16[2,640,2048,1]{2,1,3,0:T(8,128)(2,1)S(1)} %bitcast.352, bf16[2,2,2048,1024]{3,2,1,0:T(8,128)(2,1)} %param.46), kind=kOutput, calls=%fused_computation.275 | convolution fusion | flops 10737418240 | bytes 32505856 | tf_op jit(solution)/shard_map/ecd,ejdf->ejcf/dot_general | solution.py:129
  241.8 9.6 %bitcast_add_fusion.1 = f32[2,2,640,1024]{3,2,1,0:T(8,128)} fusion(f32[2,640,2,1024]{3,1,2,0:T(8,128)} %fusion.177, bf16[2,2,16,640]{3,2,1,0:T(8,128)(2,1)S(1)} %convolution_convert_fusion.3, bf16[2,2,8,16,1024]{4,3,2,1,0:T(8,128)(2,1)} %param.57, s32[]{:T(128)S(6)} %select_n.46), kind=kOutput, calls=%fused_computation.46 | convolution fusion | flops 86507520 | bytes 21184516 | tf_op jit(solution)/shard_map/ejcr,ejrf->ejcf/dot_general | solution.py:129
  251.5 16.5 %fusion.58 = (bf16[2,1,640,1024]{3,2,0,1:T(8,128)(2,1)}, bf16[2,1,640,1024]{3,2,0,1:T(8,128)(2,1)}, bf16[2,640,1024]{2,1,0:T(8,128)(2,1)}) fusion(f32[2,2,640,1024]{3,2,1,0:T(8,128)} %bitcast_add_fusion.1, f32[2,640,1024]{2,1,0:T(8,128)} %fusion.128, bf16[2,640,2048]{2,1,0:T(8,128)(2,1)} %bitcast.349, bf16[2,1024,2048]{2,1,0:T(8,128)(2,1)} %param.47, ...), kind=kOutput, calls=%fused_computation.82 | convolution fusion | flops 5390991360 | bytes 37229568 | tf_op jit(solution)/shard_map/ecd,efd->ecf/dot_general | solution.py:129
  267.9 4.0 fusion.70
  271.9 19.0 %fusion.33 = f32[2,640,2048,1]{2,1,0,3:T(8,128)} fusion(bf16[2,2,2048,1024]{3,2,1,0:T(8,128)(2,1)} %param.46, bf16[2,1,640,1024]{3,2,0,1:T(8,128)(2,1)} %get-tuple-element.290, bf16[2,1,640,1024]{3,2,0,1:T(8,128)(2,1)} %get-tuple-element.289), kind=kOutput, calls=%fused_computation.42 | convolution fusion | flops 10740039680 | bytes 32505856 | tf_op jit(solution)/shard_map/ejcf,ejdf->ecd/dot_general | solution.py:129
  290.9 5.6 fusion.35
  296.5 3.3 bitcast_convert_fusion
  299.9 51.2 %reduce-scatter.10.cloned.1.call-done = bf16[128,2048]{1,0:T(8,128)(2,1)} async-done(((bf16[1024,2048]{1,0:T(8,128)(2,1)}), bf16[128,2048]{1,0:T(8,128)(2,1)}) %reduce-scatter.10.cloned.1.call-update) | async-done | bytes 524304 | tf_op jit(solution)/shard_map/reduce_scatter | solution.py:229
  352.9 2.8 fusion.166
  356.6 2.2 convolution_convert_fusion.4
  359.5 2.5 convolution_convert_fusion.5
  362.0 3.6 convolution_convert_fusion.1
  366.4 3.3 fusion.64
  370.5 3.5 convolution_convert_fusion
  374.9 12.9 %fusion.178 = f32[2,640,2048]{2,1,0:T(8,128)} fusion(bf16[2,640,1024]{2,1,0:T(8,128)(2,1)} %get-tuple-element.291, bf16[2,1024,2048]{2,1,0:T(8,128)(2,1)} %param.47), kind=kOutput, calls=%fused_computation.276 | convolution fusion | flops 5368709120 | bytes 21495808 | tf_op jit(solution)/shard_map/ecf,efd->ecd/dot_general | solution.py:129
  388.6 3.9 all-gather.11.cloned.1.call-done
  392.5 3.5 convolution_convert_fusion.6
  402.4 20.4 %while.28 = (s32[]{:T(128)}, f32[1024,2,128]{0,2,1:T(8,128)}, f32[1024,2,128]{0,2,1:T(8,128)}, bf16[2,512,2,128]{3,2,1,0:T(2,128)(2,1)}, bf16[2,512,2,128]{3,1,2...) while((s32[]{:T(128)}, f32[1024,2,128]{0,2,1:T(8,128)}, ...), condition=%wide.region_14.15_spmd.clone, body=%wide.region_12.14_spmd.clone.sunk | while | flops 1356332032 | bytes 66875788 | solution.py:260
  422.8 2.2 stack_reshape.3
  425.0 2.8 fusion.180
  428.7 2.1 convert_element_type.260
  430.8 2.0 copy.237
  432.8 2.1 convert_element_type.262
  434.9 2.0 copy.238
  443.0 2.2 maximum_bitcast_fusion
  445.2 2.6 reshape.280
  448.0 4.8 fusion.167
  452.8 4.2 fusion.36
  457.8 8.2 %multiply_convert_fusion.1 = bf16[2,640,2048]{2,1,0:T(8,128)(2,1)} fusion(f32[2,640,2048]{2,1,0:T(8,128)} %fusion.178, f32[2,640]{1,0:T(2,128)S(1)} %copy-done.49, bf16[2,640,16]{1,2,0:T(8,128)(2,1)S(1)} %copy-done.33, bf16[2,8,16,2048]{3,2,1,0:T(8,128)(2,1)} %param.59, s32[]{:T(128)S(6)} %select_n.46), kind=kOutput, calls=%fused_computation.47 | convolution fusion | flops 91750400 | bytes 15905796 | tf_op jit(solution)/shard_map/ecr,erd->ecd/dot_general | solution.py:129
  471.0 11.2 %reduce-scatter.14.cloned.1.call-done = f32[1,64,256]{2,1,0:T(8,128)} async-done(((f32[8,64,256]{2,1,0:T(8,128)}), f32[1,64,256]{2,1,0:T(8,128)}) %reduce-scatter.14.cloned.1.call-update) | async-done | bytes 65552 | tf_op jit(solution)/shard_map/reduce_scatter | solution.py:324
  484.0 4.6 all-to-all-start
  491.2 3.2 all-to-all-done
  494.3 4.2 all-to-all-start.1
  498.8 5.9 bitcast_convert_fusion.1
  508.8 4.6 all-to-all-done.1
  519.3 2.0 copy.249
  538.4 37.4 %psum.7 = f32[]{:T(128)} all-reduce(f32[]{:T(128)S(6)} %add.297), channel_id=1, replica_groups=mesh['dp'=4,'expert'=8] {'dp','expert'}, use_global_device_ids=true, to_apply=%region_33.34 | all-reduce | flops 1 | bytes 8 | tf_op jit(solution)/shard_map/psum | solution.py:343
  578.6 2.1 add_multiply_fusion.3
  580.8 2.9 add_multiply_fusion.4
  583.7 2.4 add_multiply_fusion.2
  586.1 2.4 add_multiply_fusion.1
  588.5 3.3 add_multiply_fusion
  593.3 3.9 fusion.79
  (294 shorter events, 100.1 us)
Async XLA Ops:
  7.2 49.3 %copy-start = (bf16[3,2048,256]{2,1,0:T(8,128)(2,1)S(1)}, bf16[3,2048,256]{2,1,0:T(8,128)(2,1)}, u32[]{:S(2)}) copy-start(bf16[3,2048,256]{2,1,0:T(8,128)(2,1)} %param.44) | copy-start | bytes 9437188
  7.2 43.5 %all-gather.7.cloned.1.call-start = ((), (), s32[]{:S(2)}) async-start(), calls=%async_computation.7 | async-start | bytes 4718592 | tf_op jit(solution)/shard_map/all_gather | solution.py:133
  11.2 129.0 %reduce-scatter.6.cloned.1.call-start = ((), (), s32[]{:S(2)}) async-start(), calls=%async_computation.8 | async-start | bytes 4718592 | tf_op jit(solution)/shard_map/reduce_scatter | solution.py:178
  50.7 5.8 copy-start.4
  70.5 2.9 copy-start.12
  75.7 2.9 copy-start.12
  80.9 4.0 copy-start.55
  82.1 2.7 copy-start.50
  88.9 52.8 %copy-start.52 = (f32[2048]{0:T(1024)S(1)}, f32[2048]{0:T(1024)}, u32[]{:S(2)}) copy-start(f32[2048]{0:T(1024)} %param.43) | copy-start | bytes 24580
  88.9 55.1 %copy-start.59 = (f32[1,128,8]{1,2,0:T(8,128)S(1)}, f32[1,128,8]{1,2,0:T(8,128)}, u32[]{:S(2)}) copy-start(f32[1,128,8]{1,2,0:T(8,128)} %param.49) | copy-start | bytes 12292
  88.9 55.1 %copy-start.60 = (s32[1,128,8]{1,2,0:T(8,128)S(1)}, s32[1,128,8]{1,2,0:T(8,128)}, u32[]{:S(2)}) copy-start(s32[1,128,8]{1,2,0:T(8,128)} %param.48) | copy-start | bytes 12292
  88.9 89.8 %all-gather.13.cloned.1.call-start = ((), (), s32[]{:S(2)}) async-start(), calls=%async_computation.15 | async-start | bytes 4718592 | tf_op jit(solution)/shard_map/all_gather | solution.py:134
  89.7 128.0 %all-gather.9.cloned.1.call-start = ((), (), s32[]{:S(2)}) async-start(), calls=%async_computation.9 | async-start | bytes 4718592 | tf_op jit(solution)/shard_map/all_gather | solution.py:187
  141.7 211.1 %copy-start.57 = (f32[128]{0:T(128)}, f32[128]{0:T(128)S(1)}, u32[]{:S(2)}) copy-start(f32[128]{0:T(128)S(1)} %add_rsqrt_fusion) | copy-start | bytes 1540
  143.9 207.2 %reduce-scatter.10.cloned.1.call-start = ((), (), s32[]{:S(2)}) async-start(), calls=%async_computation.11 | async-start | bytes 4718592 | tf_op jit(solution)/shard_map/reduce_scatter | solution.py:229
  153.9 208.1 %copy-start.48 = (f32[2,640]{1,0:T(2,128)}, f32[2,640]{1,0:T(2,128)S(1)}, u32[]{:S(2)}) copy-start(f32[2,640]{1,0:T(2,128)S(1)} %mul.647) | copy-start | bytes 15364
  183.3 2.4 copy-start.2
  221.8 20.0 %copy-start.3 = (bf16[2,8,80,2048]{3,2,1,0:T(8,128)(2,1)}, bf16[2,8,80,2048]{3,2,1,0:T(8,128)(2,1)S(1)}, u32[]{:S(2)}) copy-start(bf16[2,8,80,2048]{3,2,1,0:T(8,128)(2,1)S(1)} %copy.208) | copy-start | bytes 15728644
  299.8 56.7 %copy-start.65 = (s32[4]{0:T(128)S(1)}, s32[4]{0:T(128)}, u32[]{:S(2)}) copy-start(s32[4]{0:T(128)} %param.50) | copy-start | bytes 52
  299.9 92.6 %all-gather.11.cloned.1.call-start = ((), (), s32[]{:S(2)}) async-start(), calls=%async_computation.12 | async-start | bytes 4718592 | tf_op jit(solution)/shard_map/all_gather | solution.py:234
  352.9 3.8 copy-start.63
  355.7 126.5 %reduce-scatter.14.cloned.1.call-start = ((), (), s32[]{:S(2)}) async-start(), calls=%async_computation.14 | async-start | bytes 589824 | tf_op jit(solution)/shard_map/reduce_scatter | solution.py:324
  362.0 7.7 %copy-start.32 = (bf16[2,640,16]{1,2,0:T(8,128)(2,1)}, bf16[2,640,16]{1,2,0:T(8,128)(2,1)S(1)}, u32[]{:S(2)}) copy-start(bf16[2,640,16]{1,2,0:T(8,128)(2,1)S(1)} %convolution_convert_fusion.5) | copy-start | bytes 122884
  374.9 12.9 %copy-start.31 = (bf16[64,4,512]{2,1,0:T(4,128)(2,1)S(1)}, bf16[64,4,512]{2,1,0:T(4,128)(2,1)}, u32[]{:S(2)}) copy-start(bf16[64,4,512]{2,1,0:T(4,128)(2,1)} %reshape.281) | copy-start | bytes 786436
  392.5 3.5 copy-start.11
  392.5 3.8 copy-start.28
  396.2 6.2 %copy-start.56 = (f32[2,2,512]{2,1,0:T(2,128)S(1)}, f32[2,2,512]{2,1,0:T(2,128)}, u32[]{:S(2)}) copy-start(f32[2,2,512]{2,1,0:T(2,128)} %copy-done.55) | copy-start | bytes 24580
  402.4 22.6 %copy-start.51 = (bf16[1024,16]{0,1:T(8,128)(2,1)S(1)}, bf16[1024,16]{0,1:T(8,128)(2,1)}, u32[]{:S(2)}) copy-start(bf16[1024,16]{0,1:T(8,128)(2,1)} %copy-done.50) | copy-start | bytes 98308
  402.4 3.1 copy-start.9
  408.1 1.9 copy-start.6
  408.1 1.9 copy-start.7
  409.3 1.4 copy-start.25
  412.5 3.1 copy-start.9
  418.2 1.9 copy-start.6
  418.2 1.9 copy-start.7
  419.4 1.4 copy-start.25
  437.0 2.7 copy-start.5
  447.9 4.9 copy-start.42
  447.9 143.9 %reduce-scatter.12.cloned.1.call-start = ((), (), s32[]{:S(2)}) async-start(), calls=%async_computation.13 | async-start | bytes 4718592 | tf_op jit(solution)/shard_map/reduce_scatter | solution.py:274
  457.8 8.2 %copy-start.36 = (bf16[64,4,256]{2,1,0:T(4,128)(2,1)S(1)}, bf16[64,4,256]{2,1,0:T(4,128)(2,1)}, u32[]{:S(2)}) copy-start(bf16[64,4,256]{2,1,0:T(4,128)(2,1)} %reshape.282) | copy-start | bytes 393220
  457.8 8.9 %copy-start.47 = (bf16[32,4,256]{2,1,0:T(4,128)(2,1)S(1)}, bf16[32,4,256]{2,1,0:T(4,128)(2,1)}, u32[]{:S(2)}) copy-start(bf16[32,4,256]{2,1,0:T(4,128)(2,1)} %reshape.283) | copy-start | bytes 196612
  457.8 9.6 %copy-start.35 = (bf16[32,4,512]{2,1,0:T(4,128)(2,1)S(1)}, bf16[32,4,512]{2,1,0:T(4,128)(2,1)}, u32[]{:S(2)}) copy-start(bf16[32,4,512]{2,1,0:T(4,128)(2,1)} %reshape.284) | copy-start | bytes 393220
  457.8 10.3 %copy-start.18 = (bf16[2,512,2,128]{3,2,1,0:T(2,128)(2,1)S(1)}, bf16[2,512,2,128]{3,2,1,0:T(2,128)(2,1)}, u32[]{:S(2)}) copy-start(bf16[2,512,2,128]{3,2,1,0:T(2,128)(2,1)} %get-tuple-element.117) | copy-start | bytes 1572868
  457.8 10.3 %copy-start.46 = (bf16[1024,16]{0,1:T(8,128)(2,1)S(1)}, bf16[1024,16]{0,1:T(8,128)(2,1)}, u32[]{:S(2)}) copy-start(bf16[1024,16]{0,1:T(8,128)(2,1)} %copy-done.45) | copy-start | bytes 98308
  457.8 10.7 %copy-start.44 = (bf16[3,16,1024]{2,1,0:T(8,128)(2,1)S(1)}, bf16[3,16,1024]{2,1,0:T(8,128)(2,1)}, u32[]{:S(2)}) copy-start(bf16[3,16,1024]{2,1,0:T(8,128)(2,1)} %copy-done.43) | copy-start | bytes 294916
  484.0 10.3 %all-to-all-start = ((f32[4,1,4096]{2,1,0:T(1,128)}), f32[4,1,4096]{2,1,0:T(1,128)S(1)}, u32[]{:S(2)}, u32[]{:S(2)}) async-start(f32[4,1,4096]{2,1,0:T(1,128)} %reshape.314), calls=%async_computation.5 | async-start | bytes 131072 | tf_op jit(solution)/shard_map/all_to_all | solution.py:326
  494.3 19.1 %all-to-all-start.1 = ((bf16[4,608,128]{2,1,0:T(8,128)(2,1)}), bf16[4,608,128]{2,1,0:T(8,128)(2,1)}, u32[]{:S(2)}, u32[]{:S(2)}) async-start(bf16[4,608,128]{2,1,0:T(8,128)(2,1)} %bitcast.372), calls=%async_computation.6 | async-start | bytes 1245184 | tf_op jit(solution)/shard_map/all_to_all | solution.py:305
  498.5 94.8 %reduce-scatter.8.cloned.1.call-start = ((), (), s32[]{:S(2)}) async-start(), calls=%async_computation.10 | async-start | bytes 4718592 | tf_op jit(solution)/shard_map/reduce_scatter | solution.py:209
  524.2 56.6 %copy-start.34 = (f32[8,16,64]{2,1,0:T(8,128)}, f32[8,16,64]{2,1,0:T(8,128)S(1)}, u32[]{:S(2)}) copy-start(f32[8,16,64]{2,1,0:T(8,128)S(1)} %multiply_reduce_fusion.15) | copy-start | bytes 98308
  533.6 52.4 %copy-start.24 = (f32[2,8,16,256]{3,2,1,0:T(8,128)}, f32[2,8,16,256]{3,2,1,0:T(8,128)S(1)}, u32[]{:S(2)}) copy-start(f32[2,8,16,256]{3,2,1,0:T(8,128)S(1)} %multiply_reduce_fusion.5) | copy-start | bytes 786436
  576.5 7.1 %copy-start.20 = (f32[4,8,16,256]{3,2,1,0:T(8,128)S(1)}, f32[4,8,16,256]{3,2,1,0:T(8,128)}, u32[]{:S(2)}) copy-start(f32[4,8,16,256]{3,2,1,0:T(8,128)} %copy-done.19) | copy-start | bytes 1572868
  576.6 7.1 %copy-start.37 = (f32[2,2,8,16,256]{4,3,2,1,0:T(8,128)S(1)}, f32[2,2,8,16,256]{4,3,2,1,0:T(8,128)}, u32[]{:S(2)}) copy-start(f32[2,2,8,16,256]{4,3,2,1,0:T(8,128)} %param.73) | copy-start | bytes 1572868
  576.6 7.1 %copy-start.38 = (f32[2,2,8,16,256]{4,3,2,1,0:T(8,128)S(1)}, f32[2,2,8,16,256]{4,3,2,1,0:T(8,128)}, u32[]{:S(2)}) copy-start(f32[2,2,8,16,256]{4,3,2,1,0:T(8,128)} %param.65) | copy-start | bytes 1572868
  576.6 9.5 %copy-start.22 = (f32[2,8,16,512]{3,2,1,0:T(8,128)S(1)}, f32[2,8,16,512]{3,2,1,0:T(8,128)}, u32[]{:S(2)}) copy-start(f32[2,8,16,512]{3,2,1,0:T(8,128)} %copy-done.21) | copy-start | bytes 1572868
  576.6 9.5 %copy-start.39 = (f32[2,8,16,512]{3,2,1,0:T(8,128)S(1)}, f32[2,8,16,512]{3,2,1,0:T(8,128)}, u32[]{:S(2)}) copy-start(f32[2,8,16,512]{3,2,1,0:T(8,128)} %param.75) | copy-start | bytes 1572868
  576.6 9.4 %copy-start.40 = (f32[2,8,16,512]{3,2,1,0:T(8,128)S(1)}, f32[2,8,16,512]{3,2,1,0:T(8,128)}, u32[]{:S(2)}) copy-start(f32[2,8,16,512]{3,2,1,0:T(8,128)} %param.67) | copy-start | bytes 1572868
  580.7 7.7 %copy-start.15 = (f32[4,8,16,512]{3,2,1,0:T(8,128)S(1)}, f32[4,8,16,512]{3,2,1,0:T(8,128)}, u32[]{:S(2)}) copy-start(f32[4,8,16,512]{3,2,1,0:T(8,128)} %copy-done.14) | copy-start | bytes 3145732
  580.7 7.7 %copy-start.29 = (f32[2,2,8,16,512]{4,3,2,1,0:T(8,128)S(1)}, f32[2,2,8,16,512]{4,3,2,1,0:T(8,128)}, u32[]{:S(2)}) copy-start(f32[2,2,8,16,512]{4,3,2,1,0:T(8,128)} %param.72) | copy-start | bytes 3145732
  580.7 7.7 %copy-start.30 = (f32[2,2,8,16,512]{4,3,2,1,0:T(8,128)S(1)}, f32[2,2,8,16,512]{4,3,2,1,0:T(8,128)}, u32[]{:S(2)}) copy-start(f32[2,2,8,16,512]{4,3,2,1,0:T(8,128)} %param.64) | copy-start | bytes 3145732
  588.4 3.4 copy-start.54
  588.4 4.9 copy-start.53
  588.4 4.9 copy-start.58
  588.4 4.9 copy-start.62
  588.5 4.9 copy-start.64
  (25 other events, 23.7 us)
Sparse Core Ops, SparseCore 0:
  11.3 39.2 all-gather.6
  89.1 51.1 reduce-scatter.5
  142.1 36.5 all-gather.12
  181.1 36.5 all-gather.8
  300.0 51.1 reduce-scatter.9
  355.9 36.5 all-gather.10
  448.0 34.1 reduce-scatter.13
  485.6 51.1 reduce-scatter.11
  540.2 51.7 reduce-scatter.7
